TPU v7x, 128 devices: a whole 4x4x4 slice. The times are simulated.
128 devices in a mesh: blk: 16 (over x_hi, z, core), group: 8 (over x_lo, y).
Axes of the slice: x: 4 (x_hi: 2, x_lo: 2; x = x_hi * 2 + x_lo), y: 4, z: 4, core: 2. Of those that a mesh axis runs over, the one named last changes fastest.
Arguments:
- past_clicks_hidden: bfloat16 [4096, 24, 2048], P(('blk', 'group')), may hold values from -7.5 to 7.5
- candidate_hidden_state: bfloat16 [4096, 2048], P(('blk', 'group')), may hold values from -6 to 6
- customer_tower_projection: bfloat16 [2048, 768], replicated, may hold values from -0.125 to 0.125
- candidate_tower_projection: bfloat16 [2048, 768], replicated, may hold values from -0.125 to 0.125
- score_scaling_scalar: float32 [1], replicated, may hold values from 68 to 136
- score_shift_scalar: float32 [1], replicated, may hold values from -14 to -12
- upcoming_catalog_ident: int32 [4096], P(('blk', 'group')), may hold values from 0 to 1023
- correct_batch_slot: int32 [4096], P(('blk', 'group')), may hold values from 0 to 4095, each once
Outputs:
- mean_loss: float32 [1], replicated
- item_grad: float32 [4096, 768], P(('blk', 'group'))
- grad_user_weight: float32 [2048, 768], P(('blk', 'group'))
- grad_item_weight: float32 [2048, 768], P(('blk', 'group'))
Inputs may be any that keep to these rules, and one draw needn't show every extreme that they name: `correct_batch_slot`: each row of the batch is the next item of exactly one user.
All inputs are finite; a program needn't handle non-finite values.
Results may differ from a plain program's by a relative error of at most 0.006.
Values may be sent and summed in bfloat16 or wider, within the bound.
A program may use at most 128 MiB of HBM per device.

v0:
```python
import jax
import jax.numpy as jnp
from jax import lax
from jax.sharding import PartitionSpec as P

EPS = 1e-06


def shifted(block, axis, distance):
    devices = range(lax.axis_size(axis))
    route = [((i - distance) % len(devices), i) for i in devices]
    return lax.ppermute(block, axis, route)


def side_by_side(arrays, axis, dim, along):
    both = jnp.concatenate(arrays, axis=along)
    out, at, done = (lax.all_gather(both, axis, axis=dim, tiled=True), 0, [])
    for a in arrays:
        done.append(lax.slice_in_dim(out, at, at + a.shape[along], axis=along))
        at += a.shape[along]
    return tuple(done)


def user_tower(past_clicks_hidden, customer_tower_projection):
    batch_size, positions, feat_width = past_clicks_hidden.shape
    pre_act = jnp.dot(
        past_clicks_hidden.reshape(batch_size * positions, feat_width),
        customer_tower_projection,
        preferred_element_type=jnp.float32,
    )
    pre_act = pre_act.reshape(batch_size, positions, -1)
    pooled = jnp.mean(jax.nn.silu(pre_act), axis=1)
    length = jnp.sqrt(jnp.sum(pooled * pooled, axis=1, keepdims=True) + EPS)
    return (pre_act, length, pooled / length)


def item_tower(candidate_hidden_state, candidate_tower_projection):
    pre_act = jnp.dot(
        candidate_hidden_state, candidate_tower_projection, preferred_element_type=jnp.float32
    )
    length = jnp.sqrt(jnp.sum(pre_act * pre_act, axis=1, keepdims=True) + EPS)
    return (length, pre_act / length)


def sphere_back(normed, length, grad_normed):
    radial = jnp.sum(normed * grad_normed, axis=1, keepdims=True)
    return (grad_normed - normed * radial) / length


def user_back(pre_act, length, normed, grad_normed):
    grad_pooled = sphere_back(normed, length, grad_normed) / pre_act.shape[1]
    sig_gate = jax.nn.sigmoid(pre_act)
    return (grad_pooled[:, None, :] * sig_gate * (1.0 + pre_act * (1.0 - sig_gate))).astype(
        jnp.bfloat16
    )


def pairwise_weight(
    user_embedding_rows,
    item_embedding_rows,
    per_user_target,
    item_label_matrix,
    smoothing_coefficient,
    column_offset,
):
    inner_product_matrix = lax.dot_general(
        user_embedding_rows,
        item_embedding_rows,
        (((1,), (1,)), ((), ())),
        preferred_element_type=jnp.float32,
    )
    label_signs_matrix = jnp.where(
        per_user_target[:, None] == item_label_matrix[None, :], 1.0, -1.0
    ).astype(jnp.float32)
    logit_offset_term = label_signs_matrix * (
        smoothing_coefficient * inner_product_matrix + column_offset
    )
    weight_matrix = (
        -smoothing_coefficient * label_signs_matrix * jax.nn.sigmoid(-logit_offset_term)
    ).astype(jnp.bfloat16)
    return (weight_matrix, jnp.sum(jax.nn.softplus(-logit_offset_term)))


def transposed(first_op, second_op):
    return lax.dot_general(
        first_op, second_op, (((0,), (0,)), ((), ())), preferred_element_type=jnp.float32
    )


def shards(
    past_clicks_hidden,
    candidate_hidden_state,
    customer_tower_projection,
    candidate_tower_projection,
    score_scaling_scalar,
    score_shift_scalar,
    upcoming_catalog_ident,
    correct_batch_slot,
):
    smoothing_coefficient = score_scaling_scalar[0]
    column_offset = score_shift_scalar[0]
    shard_rows = candidate_hidden_state.shape[0]
    feat_width = candidate_hidden_state.shape[1]
    emb_width = candidate_tower_projection.shape[1]
    blk_count = lax.axis_size("blk")
    group_count = lax.axis_size("group")
    group_index = lax.axis_index("group")
    every_item_index, all_positive = (
        lax.all_gather(upcoming_catalog_ident, ("blk", "group"), axis=0, tiled=True),
        lax.all_gather(correct_batch_slot, ("blk", "group"), axis=0, tiled=True),
    )
    all_targets = jnp.take(every_item_index, all_positive)
    matching_target = jnp.take(every_item_index, correct_batch_slot)
    pre_act, user_len, user_normed = user_tower(past_clicks_hidden, customer_tower_projection)
    user_embedding_rows = user_normed.astype(jnp.bfloat16)
    item_len, item_normed = item_tower(candidate_hidden_state, candidate_tower_projection)
    item_embedding_rows = item_normed.astype(jnp.bfloat16)
    empty_grad = jnp.zeros((shard_rows, emb_width), jnp.float32)
    grad_users = empty_grad
    grad_items = empty_grad
    total_loss = jnp.zeros((), jnp.float32)
    resident = (item_embedding_rows, user_embedding_rows)
    for group_hop in range(group_count):
        if group_hop > 0:
            resident = shifted((resident[0], resident[1]), "group", 1)
        group_anchor = (group_index - group_hop) % group_count
        loss_fraction = side_by_side((resident[0], resident[1]), "blk", 0, 1)
        fold_grad_users = grad_users
        fold_grad_items = grad_items
        fold_total_loss = total_loss
        offsets = jnp.arange(loss_fraction[0].shape[0], dtype=jnp.int32)
        fold_global_rows = (
            offsets // shard_rows * group_count + group_anchor
        ) * shard_rows + offsets % shard_rows
        visit_grad_users = fold_grad_users
        visiting = loss_fraction[0]
        visit_weight_matrix, visit_loss_part = pairwise_weight(
            user_embedding_rows,
            visiting,
            matching_target,
            jnp.take(every_item_index, fold_global_rows),
            smoothing_coefficient,
            column_offset,
        )
        visit_grad_users = visit_grad_users + jnp.dot(
            visit_weight_matrix, visiting, preferred_element_type=jnp.float32
        )
        fold_grad_users, fold_total_loss, fold_weight_matrix = (
            visit_grad_users,
            fold_total_loss + visit_loss_part,
            visit_weight_matrix,
        )
        visitors = loss_fraction[1]
        weight_matrix, loss_part = pairwise_weight(
            visitors,
            item_embedding_rows,
            jnp.take(all_targets, fold_global_rows),
            upcoming_catalog_ident,
            smoothing_coefficient,
            column_offset,
        )
        fold_grad_items = fold_grad_items + transposed(weight_matrix, visitors)
        grad_users = fold_grad_users
        grad_items = fold_grad_items
        total_loss = fold_total_loss
    total_loss = lax.psum(total_loss, ("blk", "group"))
    mean_loss = total_loss / (shard_rows * blk_count * group_count)
    grad_pre_user = user_back(pre_act, user_len, user_normed, grad_users)
    grad_pre_item = sphere_back(item_normed, item_len, grad_items).astype(jnp.bfloat16)
    flat_hist = past_clicks_hidden.reshape(-1, feat_width)
    flat_grad = grad_pre_user.reshape(-1, emb_width)
    user_part = transposed(flat_hist, flat_grad)
    item_part = transposed(candidate_hidden_state, grad_pre_item)
    stacked_grads = lax.psum_scatter(
        jnp.concatenate([user_part, item_part], axis=1),
        ("blk", "group"),
        scatter_dimension=0,
        tiled=True,
    )
    return (
        mean_loss.reshape(1),
        grad_items,
        stacked_grads[:, :emb_width],
        stacked_grads[:, emb_width:],
    )


def solution(mesh):
    placed = (
        P(("blk", "group"), None, None),
        P(("blk", "group"), None),
        P(),
        P(),
        P(),
        P(),
        P(("blk", "group")),
        P(("blk", "group")),
    )
    return jax.shard_map(
        shards,
        mesh=mesh,
        in_specs=placed,
        out_specs=(
            P(),
            P(("blk", "group"), None),
            P(("blk", "group"), None),
            P(("blk", "group"), None),
        ),
        check_vma=False,
    )
```

profile of v0, /device:TPU:0, one launch (start us, length us, event | category | flops | bytes accessed | tf_op | source)
XLA Modules:
  0.0 1110.9 jit_solution(9988577647635218722)
XLA Ops:
  11.0 4.3 multiply_reduce_fusion
  19.7 3.2 collective-permute-done
  26.5 5.7 collective-permute-done.2
  34.8 5.5 collective-permute-done.4
  43.2 5.6 collective-permute-done.6
  51.7 6.0 collective-permute-done.8
  60.2 67.3 %all-reduce.2 = (s32[4096]{0:T(1024)S(1)}, s32[4096]{0:T(1024)S(1)}) all-reduce(s32[4096]{0:T(1024)S(1)} %dynamic-update-slice, s32[4096]{0:T(1024)S(1)} %dynamic-update-slice.1), channel_id=1, replica_groups=mesh['blk'=16,'group'=8] {'blk','group'}, use_global_device_ids=true, to_apply=%add | all-reduce | flops 8192 | bytes 65536
  127.5 23.0 %gather_fusion.1 = s32[4096]{0:T(1024)S(1)} fusion(s32[4096]{0:T(1024)S(1)} %get-tuple-element.17, s32[4096]{0:T(1024)S(1)} %fusion.256), kind=kCustom, calls=%fused_computation.17 | custom fusion | bytes 49152 | tf_op jit(solution)/shard_map/jit(_take)/gather | solution.py:112
  155.4 4.5 collective-permute-done.10
  162.2 3.3 gather_fusion.9
  165.5 3.1 gather_fusion.8
  171.8 3.1 gather_fusion.16
  174.9 3.1 gather_fusion.7
  181.3 3.1 gather_fusion.6
  217.6 4.3 collective-permute-done.12
  261.2 40.3 %all-gather.19.cloned.1.call-done = bf16[512,1536]{1,0:T(8,128)(2,1)} async-done(((bf16[32,1536]{1,0:T(8,128)(2,1)}), bf16[512,1536]{1,0:T(8,128)(2,1)}) %all-gather.19.cloned.1.call-update) | async-done | bytes 1572880 | tf_op jit(solution)/shard_map/all_gather | solution.py:17
  308.2 40.6 %all-gather.21.cloned.1.call-done = bf16[512,1536]{1,0:T(8,128)(2,1)} async-done(((bf16[32,1536]{1,0:T(8,128)(2,1)}), bf16[512,1536]{1,0:T(8,128)(2,1)}) %all-gather.21.cloned.1.call-update) | async-done | bytes 1572880 | tf_op jit(solution)/shard_map/all_gather | solution.py:17
  355.7 40.4 %all-gather.23.cloned.1.call-done = bf16[512,1536]{1,0:T(8,128)(2,1)} async-done(((bf16[32,1536]{1,0:T(8,128)(2,1)}), bf16[512,1536]{1,0:T(8,128)(2,1)}) %all-gather.23.cloned.1.call-update) | async-done | bytes 1572880 | tf_op jit(solution)/shard_map/all_gather | solution.py:17
  400.1 4.8 convolution_bitcast_fusion.1
  407.1 3.7 convolution_bitcast_fusion
  410.8 11.3 %pad_maximum_fusion = f32[2048,1536]{0,1:T(8,128)} fusion(f32[2048,768]{0,1:T(8,128)} %convolution_bitcast_fusion, f32[2048,768]{0,1:T(8,128)} %convolution_bitcast_fusion.1), kind=kLoop, calls=%fused_computation.18 | loop fusion | flops 3145728 | bytes 25165824 | tf_op jit(solution)/shard_map/concatenate | solution.py:175
  422.1 12.7 %copy.22 = f32[2048,1536]{1,0:T(8,128)} copy(f32[2048,1536]{0,1:T(8,128)} %pad_maximum_fusion) | data formatting | bytes 25165824
  439.7 66.5 %psum.7 = f32[]{:T(128)} all-reduce(f32[]{:T(128)S(6)} %add.454), channel_id=1, replica_groups=mesh['blk'=16,'group'=8] {'blk','group'}, use_global_device_ids=true, to_apply=%region_11.13 | all-reduce | flops 1 | bytes 8 | tf_op jit(solution)/shard_map/psum | solution.py:166
  506.8 595.0 %reduce-scatter.4.cloned.1.call-done = f32[16,1536]{1,0:T(8,128)} async-done(((f32[2048,1536]{1,0:T(8,128)}), f32[16,1536]{1,0:T(8,128)}) %reduce-scatter.4.cloned.1.call-update) | async-done | bytes 98320
  (189 shorter events, 128.0 us)
Async XLA Ops:
  7.2 217.1 %all-gather.9.cloned.1.call-start = ((), (), s32[]{:S(2)}) async-start(), calls=%async_computation.1 | async-start | bytes 1671168 | tf_op jit(solution)/shard_map/all_gather | solution.py:17
  16.3 214.8 %all-gather.11.cloned.1.call-start = ((), (), s32[]{:S(2)}) async-start(), calls=%async_computation.2 | async-start | bytes 1671168 | tf_op jit(solution)/shard_map/all_gather | solution.py:17
  16.4 6.5 collective-permute-start
  18.2 6.2 collective-permute-start.1
  25.6 212.4 %all-gather.13.cloned.1.call-start = ((), (), s32[]{:S(2)}) async-start(), calls=%async_computation.3 | async-start | bytes 1671168 | tf_op jit(solution)/shard_map/all_gather | solution.py:17
  25.7 6.5 collective-permute-start.2
  25.8 6.9 collective-permute-start.3
  34.0 210.9 %all-gather.15.cloned.1.call-start = ((), (), s32[]{:S(2)}) async-start(), calls=%async_computation.4 | async-start | bytes 1671168 | tf_op jit(solution)/shard_map/all_gather | solution.py:17
  34.0 6.3 collective-permute-start.4
  34.1 6.7 collective-permute-start.5
  42.2 212.1 %all-gather.17.cloned.1.call-start = ((), (), s32[]{:S(2)}) async-start(), calls=%async_computation.5 | async-start | bytes 1671168 | tf_op jit(solution)/shard_map/all_gather | solution.py:17
  42.2 6.5 collective-permute-start.6
  42.3 6.9 collective-permute-start.7
  50.6 250.8 %all-gather.19.cloned.1.call-start = ((), (), s32[]{:S(2)}) async-start(), calls=%async_computation.6 | async-start | bytes 1671168 | tf_op jit(solution)/shard_map/all_gather | solution.py:17
  50.7 7.0 collective-permute-start.8
  50.8 7.4 collective-permute-start.9
  59.5 289.3 %all-gather.21.cloned.1.call-start = ((), (), s32[]{:S(2)}) async-start(), calls=%async_computation.7 | async-start | bytes 1671168 | tf_op jit(solution)/shard_map/all_gather | solution.py:17
  153.6 6.3 collective-permute-start.10
  153.6 6.8 collective-permute-start.11
  161.9 234.2 %all-gather.23.cloned.1.call-start = ((), (), s32[]{:S(2)}) async-start(), calls=%async_computation.8 | async-start | bytes 1671168 | tf_op jit(solution)/shard_map/all_gather | solution.py:17
  215.4 6.5 collective-permute-start.12
  215.5 7.0 collective-permute-start.13
  224.0 877.8 %reduce-scatter.4.cloned.1.call-start = ((), (), s32[]{:S(2)}) async-start(), calls=%async_computation.9 | async-start | bytes 12681216
  353.0 45.5 %copy-start.19 = (f32[32]{0:T(128)S(1)}, f32[32]{0:T(128)}, u32[]{:S(2)}) copy-start(f32[32]{0:T(128)} %copy-done.18) | copy-start | bytes 388
  (29 other events, 215.2 us)
Sparse Core Ops, SparseCore 0:
  16.5 48.5 all-gather.8
  67.5 44.9 all-gather.10
  115.0 44.8 all-gather.12
  162.2 44.8 all-gather.14
  209.4 44.8 all-gather.16
  256.6 44.8 all-gather.18
  303.9 44.8 all-gather.20
  351.3 44.8 all-gather.22
  434.9 666.8 reduce-scatter.3
where the time goes:
time: 1110 us
  waiting for transfers between devices  758 us (68%)
  blocking collectives  134 us (12%)
  local copies, waits for them, and re-layouts  93.7 us (8%)
  matrix products  69.7 us (6%)
  other arithmetic  23.5 us (2%)
  between operations  22.5 us (2%)
    unnamed x10, waiting for transfers between devices  595 us
    all_gather x8, waiting for transfers between devices, side_by_side(): out, at, done = (lax.all_gather(both, axis, axis=dim, tiled=True), 0, [])  124 us
    unnamed x1, blocking collectives  67.3 us
    psum x1, blocking collectives, shards(): total_loss = lax.psum(total_loss, ('blk', 'group'))  66.5 us
    ppermute x14, waiting for transfers between devices, shifted(): return lax.ppermute(block, axis, route)  39.4 us
    dot_general x10, matrix products, transposed(): lax.dot_general(first_op, second_op, (((0,), (0,)), ((), ())), preferred_...  29.2 us
    gather x8, local copies, waits for them, and re-layouts, shards(): jnp.take(every_item_index, fold_global_rows)  25.3 us
    gather x8, local copies, waits for them, and re-layouts, shards(): jnp.take(all_targets, fold_global_rows)  25.1 us
  transfers between devices with their start and end apart: 23, of which 19 were waited for; matrix products, arithmetic and copies ran while one was open for 12% of the time, Pallas kernels for 0%

commit v1 on v0

v1 whole, which is shorter than its diff:
```python
import functools

import jax
import jax.numpy as jnp
from jax import lax
from jax.experimental import pallas as pl
from jax.experimental.pallas import tpu as pltpu
from jax.sharding import PartitionSpec as P

EPS = 1e-06
MESH = pl.DeviceIdType.MESH
F32 = jnp.float32
BF16 = jnp.bfloat16
CORES = 2
COLOURS = 3


def dot(a, b):
    return jnp.dot(a, b, preferred_element_type=F32)


def dot_t(a, b):
    return lax.dot_general(a, b, (((0,), (0,)), ((), ())), preferred_element_type=F32)


def dot_nt(a, b):
    return lax.dot_general(a, b, (((1,), (1,)), ((), ())), preferred_element_type=F32)


def sigmoid(v):
    return 1.0 / (1.0 + jnp.exp(-v))


def tower_kernel(
    N, XL, TOTAL,
    x_hbm, ci_hbm, wu_hbm, wi_hbm, scale_ref, shift_ref, ids_ref, slot_ref,
    loss_ref, ig_ref, gu_ref, gi_ref,
    xv, xs, civ, cis, wuv, wiv, pre, pooled, gp, ulen, inorm, ilen,
    ua, ia, idbuf, slotbuf, tgtbuf, wt, pig, rig, pgu, rgu, g, gs, gi, gis,
    part, ra, sa, rb, sb, rc, losses, corelosses,
    lsem, xsem_s, xsem_r, id_s, id_r, slot_s, slot_r, tgt_s, tgt_r,
    ia_s, ia_r, ua_s, ua_r, ig_s, ig_r, ug_s, ug_r, g_s, g_r,
    rs_s, rs_r, lo_s, lo_r,
):
    USERS, E = pooled.shape
    HIST = xv.shape[0] // USERS
    FEAT = 128 if N == 4 else XL * N * 16
    QN = (N // XL) * N
    NU = N * CORES
    NI = N * N
    CW = 2 * E // COLOURS
    blk = lax.axis_index("blk")
    group = lax.axis_index("group")
    c = lax.rem(blk, CORES)
    z = lax.rem(blk // CORES, N)
    x = (blk // (CORES * N)) * XL + group // N
    y = lax.rem(group, N)

    def device(px, py, pz, pc):
        return (((px // XL) * N + pz) * CORES + pc, lax.rem(px, XL) * N + py)

    def plus(v, d, n):
        return v if d == 0 else lax.rem(v + d, n)

    def minus(v, d, n):
        return v if d == 0 else lax.rem(v + n - d, n)

    def send(src, dst, ssem, rsem, to):
        copy = pltpu.make_async_remote_copy(
            src_ref=src, dst_ref=dst, send_sem=ssem, recv_sem=rsem, device_id=to, device_id_type=MESH
        )
        copy.start()
        sent.append(copy)
        return copy

    sent = []
    sibling = device(x, y, z, 1 - c)
    user_peers = [(dy, dc) for dy in range(N) for dc in range(CORES) if (dy, dc) != (0, 0)]
    item_peers = [(dx, dz) for dx in range(N) for dz in range(N) if (dx, dz) != (0, 0)]

    def user_peer(dy, dc):
        return device(x, plus(y, dy, N), z, plus(c, dc, CORES))

    def user_slot(dy, dc):
        return plus(y, dy, N) * CORES + plus(c, dc, CORES)

    def item_peer(dx, dz):
        return device(plus(x, dx, N), y, plus(z, dz, N), c)

    load_ci = pltpu.make_async_copy(ci_hbm, civ, lsem.at[0])
    load_wi = pltpu.make_async_copy(wi_hbm, wiv, lsem.at[1])
    load_x = pltpu.make_async_copy(x_hbm, xv, lsem.at[2])
    load_wu = pltpu.make_async_copy(wu_hbm, wuv, lsem.at[3])
    for load in (load_ci, load_wi, load_x, load_wu):
        load.start()

    barrier = pltpu.get_barrier_semaphore()
    for d in user_peers:
        pl.semaphore_signal(barrier, inc=1, device_id=user_peer(*d), device_id_type=MESH)
    for d in item_peers:
        pl.semaphore_signal(barrier, inc=1, device_id=item_peer(*d), device_id_type=MESH)

    rows = lax.broadcasted_iota(jnp.int32, (USERS, USERS), 0)
    lanes = lax.broadcasted_iota(jnp.int32, (USERS, USERS), 1)
    id_col = jnp.sum(jnp.where(rows == lanes, ids_ref[...].astype(F32), 0.0), axis=1, keepdims=True)
    slot_col = jnp.sum(jnp.where(rows == lanes, slot_ref[...].astype(F32), 0.0), axis=1, keepdims=True)
    idbuf[0] = jnp.broadcast_to(id_col, (USERS, 128))
    my_user_slot = y * CORES + c
    wide_rows = lax.broadcasted_iota(jnp.int32, (USERS, NU * USERS), 0)
    wide_lanes = lax.broadcasted_iota(jnp.int32, (USERS, NU * USERS), 1)
    slot_row = jnp.sum(
        jnp.where(wide_lanes == wide_rows + my_user_slot * USERS, slot_col, 0.0), axis=0, keepdims=True
    )
    slotbuf[0] = jnp.broadcast_to(slot_row, (8, NU * USERS))

    pl.semaphore_wait(barrier, len(user_peers) + len(item_peers))

    id_recv, slot_recv = [], []
    for n, d in enumerate(user_peers):
        slot_recv.append(send(slotbuf.at[0], slotbuf.at[n + 1], slot_s.at[n], slot_r.at[n], user_peer(*d)))
    for n, (dx, dz) in enumerate(item_peers):
        s = dx * N + dz
        id_recv.append(send(idbuf.at[0], idbuf.at[s], id_s.at[n], id_r.at[n], item_peer(dx, dz)))

    load_ci.wait()
    load_wi.wait()
    item_pre = dot(civ[...], wiv[...])
    item_len = jnp.sqrt(jnp.sum(item_pre * item_pre, axis=1, keepdims=True) + EPS)
    item_normed = item_pre / item_len
    inorm[...] = item_normed
    ilen[...] = jnp.broadcast_to(item_len, (USERS, 128))
    ia[0] = item_normed.astype(BF16)
    ia_recv = []
    for n, (dx, dz) in enumerate(item_peers):
        s = dx * N + dz
        ia_recv.append(send(ia.at[0], ia.at[s], ia_s.at[n], ia_r.at[n], item_peer(dx, dz)))

    load_x.wait()
    x_recv = []
    for q in range(QN):
        cols = pl.ds(pl.multiple_of((q * CORES + 1 - c) * FEAT, FEAT), FEAT)
        x_recv.append(send(xv.at[:, cols], xs.at[q], xsem_s.at[q], xsem_r.at[q], sibling))
        x_recv.append(send(civ.at[:, cols], cis.at[q], xsem_s.at[QN + q], xsem_r.at[QN + q], sibling))
    load_wu.wait()

    def forward(n, _):
        cols = pl.ds(pl.multiple_of(n * 256, 256), 256)
        pre[:, cols] = dot(xv[...], wuv[:, cols])
        return 0

    lax.fori_loop(0, E // 256, forward, 0)

    def pool(n, _):
        u = n // (E // 128)
        j = lax.rem(n, E // 128)
        cols = pl.ds(pl.multiple_of(j * 128, 128), 128)
        v = pre[pl.ds(pl.multiple_of(u * 8 * HIST, 8 * HIST), 8 * HIST), cols]
        act = v * sigmoid(v)
        pooled[pl.ds(pl.multiple_of(u * 8, 8), 8), cols] = jnp.sum(act.reshape(8, HIST, 128), axis=1) / HIST
        return 0

    lax.fori_loop(0, (USERS // 8) * (E // 128), pool, 0)
    mean = pooled[...]
    user_len = jnp.sqrt(jnp.sum(mean * mean, axis=1, keepdims=True) + EPS)
    user_normed = mean / user_len
    ulen[...] = jnp.broadcast_to(user_len, (USERS, 128))
    pooled[...] = user_normed
    ua[my_user_slot] = user_normed.astype(BF16)
    ua_recv = []
    for n, d in enumerate(user_peers):
        ua_recv.append(send(ua.at[my_user_slot], ua.at[my_user_slot], ua_s.at[n], ua_r.at[n], user_peer(*d)))

    for copy in slot_recv + id_recv:
        copy.wait_recv()
    slots = slotbuf[0]
    for n in range(1, NU):
        slots = slots + slotbuf[n]
    slots = slots[0:1]
    found = jnp.zeros((1, NU * USERS), F32)
    item_rows = lax.broadcasted_iota(jnp.int32, (USERS, 128), 0)
    for dx in range(N):
        for dz in range(N):
            ox, oz = minus(x, dx, N), minus(z, dz, N)
            ob, og = device(ox, y, oz, c)
            at = (item_rows + (ob * (XL * N) + og) * USERS).astype(F32)
            ids = idbuf[dx * N + dz]
            wide = NU * USERS // 128
            hit = jnp.concatenate([at] * wide, axis=1) == slots
            found = found + jnp.sum(
                jnp.where(hit, jnp.concatenate([ids] * wide, axis=1), 0.0), axis=0, keepdims=True
            )
    tgtbuf[0] = jnp.broadcast_to(found, (8, NU * USERS))
    tgt_recv = []
    for n, d in enumerate(user_peers):
        tgt_recv.append(send(tgtbuf.at[0], tgtbuf.at[n + 1], tgt_s.at[n], tgt_r.at[n], user_peer(*d)))
    for copy in tgt_recv:
        copy.wait_recv()
    targets = tgtbuf[0]
    for n in range(1, NU):
        targets = targets + tgtbuf[n]
    targets = targets[0:1]

    for copy in ua_recv + ia_recv:
        copy.wait_recv()
    scale = scale_ref[0]
    shift = shift_ref[0]
    users = ua[...].reshape(NU * USERS, E)
    loss = jnp.zeros((8, 128), F32)
    ig_recv = []
    peer_at = {d: n for n, d in enumerate(item_peers)}
    for dx in range(N):
        items = ia[dx * N:(dx + 1) * N].reshape(N * USERS, E)
        scores = dot_nt(items, users)
        wide = NU * USERS // 128
        ids = idbuf[dx * N:(dx + 1) * N].reshape(N * USERS, 128)
        sign = jnp.where(jnp.concatenate([ids] * wide, axis=1) == targets, 1.0, -1.0)
        margin = sign * (scale * scores + shift)
        e = jnp.exp(-jnp.abs(margin))
        terms = jnp.log1p(e) + jnp.maximum(-margin, 0.0)
        gate = jnp.where(margin >= 0.0, e, 1.0) / (1.0 + e)
        weights = (-scale * sign * gate).astype(BF16)
        wt[dx * N * USERS:(dx + 1) * N * USERS, :] = weights
        terms = jnp.sum(terms.reshape(N * USERS // 8, 8, NU * USERS), axis=0)
        for j in range(wide):
            loss = loss + terms[:, j * 128:(j + 1) * 128]
        pig[dx * N:(dx + 1) * N] = dot(weights, users).astype(BF16).reshape(N, USERS, E)
        for dz in range(N):
            if (dx, dz) == (0, 0):
                continue
            n = peer_at[(dx, dz)]
            to = device(minus(x, dx, N), y, minus(z, dz, N), c)
            ig_recv.append(send(pig.at[dx * N + dz], rig.at[n], ig_s.at[n], ig_r.at[n], to))
    pgu[...] = dot_t(wt[...], ia[...].reshape(NI * USERS, E)).astype(BF16).reshape(NU, USERS, E)
    ug_recv = []
    for n, (dy, dc) in enumerate(user_peers):
        s = user_slot(dy, dc)
        ug_recv.append(send(pgu.at[s], rgu.at[n], ug_s.at[n], ug_r.at[n], user_peer(dy, dc)))

    def reduce_loss(value, step, pos):
        losses[step, pos] = value
        copies = []
        for d in range(1, N):
            at = [x, y, z]
            at[step] = plus(pos, d, N)
            copies.append(
                send(losses.at[step, pos], losses.at[step, pos], lo_s.at[step, d - 1], lo_r.at[step, d - 1],
                     device(at[0], at[1], at[2], c))
            )
        return copies

    def reduced_loss(step):
        total = losses[step, 0]
        for d in range(1, N):
            total = total + losses[step, d]
        return total

    loss_copies = reduce_loss(loss, 0, x)

    for copy in ig_recv:
        copy.wait_recv()
    item_grad = pig[0].astype(F32)
    for n in range(len(item_peers)):
        item_grad = item_grad + rig[n].astype(F32)
    ig_ref[...] = item_grad
    item_normed = inorm[...]
    radial = jnp.sum(item_normed * item_grad, axis=1, keepdims=True)
    gi[...] = ((item_grad - item_normed * radial) / ilen[:, 0:1]).astype(BF16)
    gi_copy = send(gi, gis, g_s.at[1], g_r.at[1], sibling)

    for copy in loss_copies:
        copy.wait_recv()
    loss_copies = reduce_loss(reduced_loss(0), 1, y)

    for copy in ug_recv:
        copy.wait_recv()
    grad_users = pgu[my_user_slot].astype(F32)
    for n in range(len(user_peers)):
        grad_users = grad_users + rgu[n].astype(F32)
    user_normed = pooled[...]
    radial = jnp.sum(user_normed * grad_users, axis=1, keepdims=True)
    gp[...] = (grad_users - user_normed * radial) / ulen[:, 0:1] / HIST

    def backward(n, _):
        u = n // (E // 128)
        j = lax.rem(n, E // 128)
        cols = pl.ds(pl.multiple_of(j * 128, 128), 128)
        at = pl.ds(pl.multiple_of(u * 8 * HIST, 8 * HIST), 8 * HIST)
        v = pre[at, cols]
        s = sigmoid(v)
        outer = jnp.broadcast_to(gp[pl.ds(pl.multiple_of(u * 8, 8), 8), cols][:, None, :], (8, HIST, 128))
        g[at, cols] = (outer.reshape(8 * HIST, 128) * s * (1.0 + v * (1.0 - s))).astype(BF16)
        return 0

    lax.fori_loop(0, (USERS // 8) * (E // 128), backward, 0)
    g_copy = send(g, gs, g_s.at[0], g_r.at[0], sibling)

    for copy in loss_copies:
        copy.wait_recv()
    loss_copies = reduce_loss(reduced_loss(1), 2, z)

    for copy in x_recv:
        copy.wait_recv()
    gi_copy.wait_recv()

    pos = (x, y, z)

    def put(k, q, r):
        r = r.astype(BF16)
        xh, qz = q // N, lax.rem(q, N)
        for xl in range(XL):
            for yy in range(N):
                at = (xh * XL + xl, yy, qz)
                i0, i1, i2 = at[k % 3], at[(k + 1) % 3], at[(k + 2) % 3]
                o = (xl * N + yy) * 16
                part[k, i0, i1, i2] = r[o:o + 16]

    def own_cols(q):
        return pl.ds(pl.multiple_of((q * CORES + c) * FEAT, FEAT), FEAT)

    def item_part(q, lo, hi):
        return dot_t(civ[:, own_cols(q)], gi[:, lo:hi]) + dot_t(cis[q], gis[:, lo:hi])

    def user_part(q, lo, hi):
        return dot_t(xv[:, own_cols(q)], g[:, lo:hi]) + dot_t(xs[q], gs[:, lo:hi])

    def colour2(q, _):
        put(2, q, item_part(q, 2 * CW - E, E))
        return 0

    def colour1(q, _):
        put(1, q, jnp.concatenate([user_part(q, CW, E), item_part(q, 0, 2 * CW - E)], axis=1))
        return 0

    def colour0(q, _):
        put(0, q, user_part(q, 0, CW))
        return 0

    def towards(axis, v):
        at = list(pos)
        at[axis] = v
        return device(at[0], at[1], at[2], c)

    def phase(k, ph, src, dst):
        axis = (k + ph) % 3
        copies = []
        for d in range(1, N):
            t = plus(pos[axis], d, N)
            copies.append(
                send(src.at[k, t], dst.at[k, d - 1], rs_s.at[k, ph, d - 1], rs_r.at[k, ph, d - 1], towards(axis, t))
            )
        return copies

    lax.fori_loop(0, QN, colour2, 0)
    flight = {2: phase(2, 0, part, ra)}
    for copy in loss_copies:
        copy.wait_recv()
    loss = reduced_loss(2)
    corelosses[c] = loss
    core_copy = send(corelosses.at[c], corelosses.at[c], lo_s.at[3, 0], lo_r.at[3, 0], sibling)
    g_copy.wait_recv()
    lax.fori_loop(0, QN, colour1, 0)
    flight[1] = phase(1, 0, part, ra)
    lax.fori_loop(0, QN, colour0, 0)
    flight[0] = phase(0, 0, part, ra)
    core_copy.wait_recv()
    loss_ref[0] = jnp.sum(corelosses[0] + corelosses[1]) / TOTAL

    order = (2, 1, 0)
    for k in order:
        for copy in flight[k]:
            copy.wait_recv()
        me = pos[k % 3]

        def add_a(n, _, k=k, me=me):
            i, j = n // N, lax.rem(n, N)
            total = part[k, me, i, j].astype(F32)
            for d in range(N - 1):
                total = total + ra[k, d, i, j].astype(F32)
            sa[k, i, j] = total.astype(BF16)
            return 0

        lax.fori_loop(0, N * N, add_a, 0)
        flight[k] = phase(k, 1, sa, rb)
    for k in order:
        for copy in flight[k]:
            copy.wait_recv()
        me = pos[(k + 1) % 3]
        for j in range(N):
            total = sa[k, me, j].astype(F32)
            for d in range(N - 1):
                total = total + rb[k, d, j].astype(F32)
            sb[k, j] = total.astype(BF16)
        flight[k] = phase(k, 2, sb, rc)
    for k in order:
        for copy in flight[k]:
            copy.wait_recv()
        me = pos[(k + 2) % 3]
        total = sb[k, me].astype(F32)
        for d in range(N - 1):
            total = total + rc[k, d].astype(F32)
        if k == 0:
            gu_ref[:, 0:CW] = total
        elif k == 1:
            gu_ref[:, CW:E] = total[:, 0:E - CW]
            gi_ref[:, 0:2 * CW - E] = total[:, E - CW:CW]
        else:
            gi_ref[:, 2 * CW - E:E] = total
    for copy in sent:
        copy.wait_send()


def shards(N, XL, past, cand, wu, wi, scale, shift, ids, slots):
    users, hist, depth = past.shape
    E = wu.shape[1]
    total = users * lax.axis_size("blk") * lax.axis_size("group")
    NU, NI, QN = N * CORES, N * N, (N // XL) * N
    feat = depth // (QN * CORES)
    hbm = pl.BlockSpec(memory_space=pl.ANY)
    smem = pl.BlockSpec(memory_space=pltpu.SMEM)
    vmem = pl.BlockSpec(memory_space=pltpu.VMEM)
    rows = depth // (NI * N * CORES)
    CW = 2 * E // COLOURS

    def dma(*shape):
        return pltpu.SemaphoreType.DMA(shape)

    V = pltpu.VMEM
    scratch = [
        V((users * hist, depth), BF16), V((QN, users * hist, feat), BF16),
        V((users, depth), BF16), V((QN, users, feat), BF16),
        V((depth, E), BF16), V((depth, E), BF16),
        V((users * hist, E), F32), V((users, E), F32), V((users, E), F32), V((users, 128), F32),
        V((users, E), F32), V((users, 128), F32),
        V((NU, users, E), BF16), V((NI, users, E), BF16), V((NI, users, 128), F32),
        V((NU, 8, NU * users), F32), V((NU, 8, NU * users), F32),
        V((NI * users, NU * users), BF16),
        V((NI, users, E), BF16), V((NI - 1, users, E), BF16),
        V((NU, users, E), BF16), V((NU - 1, users, E), BF16),
        V((users * hist, E), BF16), V((users * hist, E), BF16), V((users, E), BF16), V((users, E), BF16),
        V((COLOURS, N, N, N, rows, CW), BF16), V((COLOURS, N - 1, N, N, rows, CW), BF16),
        V((COLOURS, N, N, rows, CW), BF16), V((COLOURS, N - 1, N, rows, CW), BF16),
        V((COLOURS, N, rows, CW), BF16), V((COLOURS, N - 1, rows, CW), BF16),
        V((3, N, 8, 128), F32), V((CORES, 8, 128), F32),
        dma(4), dma(2 * QN), dma(2 * QN), dma(NI - 1), dma(NI - 1), dma(NU - 1), dma(NU - 1),
        dma(NU - 1), dma(NU - 1), dma(NI - 1), dma(NI - 1), dma(NU - 1), dma(NU - 1),
        dma(NI - 1), dma(NI - 1), dma(NU - 1), dma(NU - 1), dma(2), dma(2),
        dma(COLOURS, 3, N - 1), dma(COLOURS, 3, N - 1), dma(4, N - 1), dma(4, N - 1),
    ]
    return pl.pallas_call(
        functools.partial(tower_kernel, N, XL, total),
        name="two_tower",
        out_shape=(
            jax.ShapeDtypeStruct((1,), F32),
            jax.ShapeDtypeStruct((users, E), F32),
            jax.ShapeDtypeStruct((rows, E), F32),
            jax.ShapeDtypeStruct((rows, E), F32),
        ),
        in_specs=[hbm, hbm, hbm, hbm, smem, smem, vmem, vmem],
        out_specs=(smem, vmem, vmem, vmem),
        scratch_shapes=scratch,
        compiler_params=pltpu.CompilerParams(
            collective_id=0, has_side_effects=True, vmem_limit_bytes=60 * 1024 * 1024
        ),
    )(
        past.reshape(users * hist, depth), cand, wu, wi, scale, shift,
        ids.reshape(1, users), slots.reshape(1, users),
    )


def solution(mesh):
    group = mesh.shape["group"]
    n = {128: 4, 16: 2}[mesh.size]
    both = ("blk", "group")
    return jax.shard_map(
        functools.partial(shards, n, group // n),
        mesh=mesh,
        in_specs=(P(both, None, None), P(both, None), P(), P(), P(), P(), P(both), P(both)),
        out_specs=(P(), P(both, None), P(both, None), P(both, None)),
        check_vma=False,
    )
```

time: 1110 us -> 83.8 us (0.08)
  waiting for transfers between devices: 758 us -> 0 us
  blocking collectives: 134 us -> 0 us
  local copies, waits for them, and re-layouts: 93.7 us -> 4.38 us
  Pallas kernels: 0 us -> 75.4 us
  matrix products: 69.7 us -> 0 us
  other arithmetic: 23.5 us -> 0 us
  between operations: 22.5 us -> 3.7 us
    unnamed x10 -> x0, waiting for transfers between devices: 595 us -> none
    all_gather x8 -> x0, waiting for transfers between devices: 124 us -> none  [side_by_side(): out, at, done = (lax.all_gather(both, axis, axis=dim, tiled=True), 0, [])]
    pallas_call x0 -> x1, Pallas kernels: none -> 75.4 us  [shards(): pl.pallas_call(functools.partial(tower_kernel, N, XL, total), name='two_t...]
    gather x18 -> x0, local copies, waits for them, and re-layouts: 74.7 us -> none  [the longest x8 25.3 us: shards(): jnp.take(every_item_index, fold_global_rows)]
    dot_general x28 -> x0, matrix products: 69.7 us -> none  [the longest x10 29.2 us: transposed(): lax.dot_general(first_op, second_op, (((0,), (0,)), ((), ())), preferred_...]
    unnamed x1 -> x0, blocking collectives: 67.3 us -> none
    psum x1 -> x0, blocking collectives: 66.5 us -> none  [shards(): total_loss = lax.psum(total_loss, ('blk', 'group'))]
    ppermute x14 -> x0, waiting for transfers between devices: 39.4 us -> none  [shifted(): return lax.ppermute(block, axis, route)]
  transfers between devices with their start and end apart: 23 -> 0, of which waited for: 19 -> 0; matrix products, arithmetic and copies ran while one was open for 12% -> 0% of each run, Pallas kernels for 0% -> 0%
where the time goes in v1:
time: 83.8 us; the launch traced here: 83.5 us
  Pallas kernels  75.4 us (90%)
  local copies, waits for them, and re-layouts  4.38 us (5%)
  between operations  3.7 us (4%)
    pallas_call x1, Pallas kernels, shards(): pl.pallas_call(functools.partial(tower_kernel, N, XL, total), name='two_t...  75.4 us
    unnamed x3, local copies, waits for them, and re-layouts  4.38 us

profile of v1, /device:TPU:0, one launch (start us, length us, event | category | flops | bytes accessed | tf_op | source)
XLA Modules:
  0.0 83.5 jit_solution(17086543072857132057)
XLA Ops:
  1.9 75.4 %two_tower.1 = (f32[1]{0:T(128)}, f32[32,768]{1,0:T(8,128)}, f32[16,768]{1,0:T(8,128)}, f32[16,768]{1,0:T(8,128)}) custom-call(bf16[768,2048]{1,0:T(8,128)(2,1)} %bitcast.3, bf16[32,2048]{1,0:T(8,128)(2,1)} %ci_hbm.1, bf16[2048,768]{1,0:T(8,128)(2,1)} %wu_hbm.1, bf16[2048,768]{1,0:T(8,128)(2,1)} %wi_hbm.1, f32[1]{0:T(128)S(6)} %copy.16.scale_ref, ...), custom_call_target="tpu_custom_call" | custom-call | tf_op jit(solution)/shard_map/two_tower/pallas_call | solution.py:449
  78.0 1.5 %copy.19 = f32[32,768]{1,0:T(8,128)} copy(f32[32,768]{1,0:T(8,128)} %get-tuple-element.9) | data formatting | bytes 196608
  79.5 1.4 %copy.20 = f32[16,768]{1,0:T(8,128)} copy(f32[16,768]{1,0:T(8,128)} %get-tuple-element.10) | data formatting | bytes 98304
  80.9 1.4 %copy.21 = f32[16,768]{1,0:T(8,128)} copy(f32[16,768]{1,0:T(8,128)} %get-tuple-element.11) | data formatting | bytes 98304

commit v2 on v1

--- a/solution.py
+++ b/solution.py
@@ -35,12 +35,12 @@
     N, XL, TOTAL,
     x_hbm, ci_hbm, wu_hbm, wi_hbm, scale_ref, shift_ref, ids_ref, slot_ref,
     loss_ref, ig_ref, gu_ref, gi_ref,
-    xv, xs, civ, cis, wuv, wiv, pre, pooled, gp, ulen, inorm, ilen,
-    ua, ia, idbuf, slotbuf, tgtbuf, wt, pig, rig, pgu, rgu, g, gs, gi, gis,
-    part, ra, sa, rb, sb, rc, losses, corelosses,
-    lsem, xsem_s, xsem_r, id_s, id_r, slot_s, slot_r, tgt_s, tgt_r,
-    ia_s, ia_r, ua_s, ua_r, ig_s, ig_r, ug_s, ug_r, g_s, g_r,
-    rs_s, rs_r, lo_s, lo_r,
+    xv, xs, civ, wuv, wiv, pre, pooled, gp, ulen, inorm, ilen,
+    ua, ia, idbuf, slotbuf, tgtbuf, wt, pig, rig, pgu, rgu, g, gi, xi, xt,
+    part, ra, sa, rb, sb, rc, parti, ri, losses, corelosses, scale_s, shift_s, idv, slotv,
+    lsem, xsem_s, xsem_r, xi_s, xi_r, id_s, id_r, slot_s, slot_r, tgt_s, tgt_r,
+    ia_s, ia_r, ua_s, ua_r, ig_s, ig_r, ug_s, ug_r, g_s, g_r, gi_s, gi_r,
+    rs_s, rs_r, ri_s, ri_r, lo_s, lo_r,
 ):
     USERS, E = pooled.shape
     HIST = xv.shape[0] // USERS
@@ -48,7 +48,9 @@
     QN = (N // XL) * N
     NU = N * CORES
     NI = N * N
-    CW = 2 * E // COLOURS
+    CW = E // COLOURS
+    XH = N // XL
+    ROWS = USERS * HIST
     blk = lax.axis_index("blk")
     group = lax.axis_index("group")
     c = lax.rem(blk, CORES)
@@ -77,6 +79,8 @@
     sibling = device(x, y, z, 1 - c)
     user_peers = [(dy, dc) for dy in range(N) for dc in range(CORES) if (dy, dc) != (0, 0)]
     item_peers = [(dx, dz) for dx in range(N) for dz in range(N) if (dx, dz) != (0, 0)]
+    feat_peers = [(dz, dc) for dz in range(N) for dc in range(CORES) if (dz, dc) != (0, 0)]
+    row_peers = [(dx, dy) for dx in range(N) for dy in range(N) if (dx, dy) != (0, 0)]
 
     def user_peer(dy, dc):
         return device(x, plus(y, dy, N), z, plus(c, dc, CORES))
@@ -87,6 +91,18 @@
     def item_peer(dx, dz):
         return device(plus(x, dx, N), y, plus(z, dz, N), c)
 
+    def feat_peer(dz, dc):
+        return device(x, y, plus(z, dz, N), plus(c, dc, CORES))
+
+    def row_peer(dx, dy):
+        return device(plus(x, dx, N), plus(y, dy, N), z, c)
+
+    small = [
+        pltpu.make_async_copy(a, b, lsem.at[4 + n])
+        for n, (a, b) in enumerate(((ids_ref, idv), (slot_ref, slotv), (scale_ref, scale_s), (shift_ref, shift_s)))
+    ]
+    for load in small:
+        load.start()
     load_ci = pltpu.make_async_copy(ci_hbm, civ, lsem.at[0])
     load_wi = pltpu.make_async_copy(wi_hbm, wiv, lsem.at[1])
     load_x = pltpu.make_async_copy(x_hbm, xv, lsem.at[2])
@@ -99,11 +115,19 @@
         pl.semaphore_signal(barrier, inc=1, device_id=user_peer(*d), device_id_type=MESH)
     for d in item_peers:
         pl.semaphore_signal(barrier, inc=1, device_id=item_peer(*d), device_id_type=MESH)
+    far_feat = [d for d in feat_peers if d[0] and d[1]]
+    far_row = [d for d in row_peers if d[0] and d[1]]
+    for d in far_feat:
+        pl.semaphore_signal(barrier, inc=1, device_id=feat_peer(*d), device_id_type=MESH)
+    for d in far_row:
+        pl.semaphore_signal(barrier, inc=1, device_id=row_peer(*d), device_id_type=MESH)
+    for load in small:
+        load.wait()
 
     rows = lax.broadcasted_iota(jnp.int32, (USERS, USERS), 0)
     lanes = lax.broadcasted_iota(jnp.int32, (USERS, USERS), 1)
-    id_col = jnp.sum(jnp.where(rows == lanes, ids_ref[...].astype(F32), 0.0), axis=1, keepdims=True)
-    slot_col = jnp.sum(jnp.where(rows == lanes, slot_ref[...].astype(F32), 0.0), axis=1, keepdims=True)
+    id_col = jnp.sum(jnp.where(rows == lanes, idv[...].astype(F32), 0.0), axis=1, keepdims=True)
+    slot_col = jnp.sum(jnp.where(rows == lanes, slotv[...].astype(F32), 0.0), axis=1, keepdims=True)
     idbuf[0] = jnp.broadcast_to(id_col, (USERS, 128))
     my_user_slot = y * CORES + c
     wide_rows = lax.broadcasted_iota(jnp.int32, (USERS, NU * USERS), 0)
@@ -113,7 +137,7 @@
     )
     slotbuf[0] = jnp.broadcast_to(slot_row, (8, NU * USERS))
 
-    pl.semaphore_wait(barrier, len(user_peers) + len(item_peers))
+    pl.semaphore_wait(barrier, len(user_peers) + len(item_peers) + len(far_feat) + len(far_row))
 
     id_recv, slot_recv = [], []
     for n, d in enumerate(user_peers):
@@ -140,7 +164,14 @@
     for q in range(QN):
         cols = pl.ds(pl.multiple_of((q * CORES + 1 - c) * FEAT, FEAT), FEAT)
         x_recv.append(send(xv.at[:, cols], xs.at[q], xsem_s.at[q], xsem_r.at[q], sibling))
-        x_recv.append(send(civ.at[:, cols], cis.at[q], xsem_s.at[QN + q], xsem_r.at[QN + q], sibling))
+    xi_recv = []
+    for n, (dz, dc) in enumerate(feat_peers):
+        pz, pc = plus(z, dz, N), plus(c, dc, CORES)
+        for h in range(XH):
+            cols = pl.ds(pl.multiple_of(((h * N + pz) * CORES + pc) * FEAT, FEAT), FEAT)
+            xi_recv.append(
+                send(civ.at[:, cols], xi.at[h, n + 1], xi_s.at[n, h], xi_r.at[n, h], feat_peer(dz, dc))
+            )
     load_wu.wait()
 
     def forward(n, _):
@@ -170,6 +201,19 @@
     for n, d in enumerate(user_peers):
         ua_recv.append(send(ua.at[my_user_slot], ua.at[my_user_slot], ua_s.at[n], ua_r.at[n], user_peer(*d)))
 
+    for h in range(XH):
+        xi[h, 0] = civ[:, pl.ds(pl.multiple_of(((h * N + z) * CORES + c) * FEAT, FEAT), FEAT)]
+    for copy in x_recv:
+        copy.wait_recv()
+
+    def turn(q, _):
+        cols = pl.ds(pl.multiple_of((q * CORES + c) * FEAT, FEAT), FEAT)
+        to = pl.ds(pl.multiple_of(q * FEAT, FEAT), FEAT)
+        xt[to, 0:ROWS] = xv[:, cols].T
+        xt[to, ROWS:2 * ROWS] = xs[q].T
+        return 0
+
+    lax.fori_loop(0, QN, turn, 0)
     for copy in slot_recv + id_recv:
         copy.wait_recv()
     slots = slotbuf[0]
@@ -202,39 +246,41 @@
 
     for copy in ua_recv + ia_recv:
         copy.wait_recv()
-    scale = scale_ref[0]
-    shift = shift_ref[0]
+    scale = scale_s[0]
+    shift = shift_s[0]
     users = ua[...].reshape(NU * USERS, E)
     loss = jnp.zeros((8, 128), F32)
-    ig_recv = []
-    peer_at = {d: n for n, d in enumerate(item_peers)}
+    wide = NU * USERS // 128
     for dx in range(N):
         items = ia[dx * N:(dx + 1) * N].reshape(N * USERS, E)
         scores = dot_nt(items, users)
-        wide = NU * USERS // 128
         ids = idbuf[dx * N:(dx + 1) * N].reshape(N * USERS, 128)
         sign = jnp.where(jnp.concatenate([ids] * wide, axis=1) == targets, 1.0, -1.0)
         margin = sign * (scale * scores + shift)
         e = jnp.exp(-jnp.abs(margin))
         terms = jnp.log1p(e) + jnp.maximum(-margin, 0.0)
         gate = jnp.where(margin >= 0.0, e, 1.0) / (1.0 + e)
-        weights = (-scale * sign * gate).astype(BF16)
-        wt[dx * N * USERS:(dx + 1) * N * USERS, :] = weights
+        wt[dx * N * USERS:(dx + 1) * N * USERS, :] = (-scale * sign * gate).astype(BF16)
         terms = jnp.sum(terms.reshape(N * USERS // 8, 8, NU * USERS), axis=0)
         for j in range(wide):
             loss = loss + terms[:, j * 128:(j + 1) * 128]
-        pig[dx * N:(dx + 1) * N] = dot(weights, users).astype(BF16).reshape(N, USERS, E)
+    pgu[...] = dot_t(wt[...], ia[...].reshape(NI * USERS, E)).astype(BF16).reshape(NU, USERS, E)
+    ug_recv = []
+    for n, (dy, dc) in enumerate(user_peers):
+        s = user_slot(dy, dc)
+        ug_recv.append(send(pgu.at[s], rgu.at[n], ug_s.at[n], ug_r.at[n], user_peer(dy, dc)))
+    ig_recv = []
+    peer_at = {d: n for n, d in enumerate(item_peers)}
+    for dx in range(N):
+        pig[dx * N:(dx + 1) * N] = (
+            dot(wt[dx * N * USERS:(dx + 1) * N * USERS, :], users).astype(BF16).reshape(N, USERS, E)
+        )
         for dz in range(N):
             if (dx, dz) == (0, 0):
                 continue
             n = peer_at[(dx, dz)]
             to = device(minus(x, dx, N), y, minus(z, dz, N), c)
             ig_recv.append(send(pig.at[dx * N + dz], rig.at[n], ig_s.at[n], ig_r.at[n], to))
-    pgu[...] = dot_t(wt[...], ia[...].reshape(NI * USERS, E)).astype(BF16).reshape(NU, USERS, E)
-    ug_recv = []
-    for n, (dy, dc) in enumerate(user_peers):
-        s = user_slot(dy, dc)
-        ug_recv.append(send(pgu.at[s], rgu.at[n], ug_s.at[n], ug_r.at[n], user_peer(dy, dc)))
 
     def reduce_loss(value, step, pos):
         losses[step, pos] = value
@@ -256,21 +302,6 @@
 
     loss_copies = reduce_loss(loss, 0, x)
 
-    for copy in ig_recv:
-        copy.wait_recv()
-    item_grad = pig[0].astype(F32)
-    for n in range(len(item_peers)):
-        item_grad = item_grad + rig[n].astype(F32)
-    ig_ref[...] = item_grad
-    item_normed = inorm[...]
-    radial = jnp.sum(item_normed * item_grad, axis=1, keepdims=True)
-    gi[...] = ((item_grad - item_normed * radial) / ilen[:, 0:1]).astype(BF16)
-    gi_copy = send(gi, gis, g_s.at[1], g_r.at[1], sibling)
-
-    for copy in loss_copies:
-        copy.wait_recv()
-    loss_copies = reduce_loss(reduced_loss(0), 1, y)
-
     for copy in ug_recv:
         copy.wait_recv()
     grad_users = pgu[my_user_slot].astype(F32)
@@ -280,60 +311,23 @@
     radial = jnp.sum(user_normed * grad_users, axis=1, keepdims=True)
     gp[...] = (grad_users - user_normed * radial) / ulen[:, 0:1] / HIST
 
-    def backward(n, _):
-        u = n // (E // 128)
-        j = lax.rem(n, E // 128)
-        cols = pl.ds(pl.multiple_of(j * 128, 128), 128)
-        at = pl.ds(pl.multiple_of(u * 8 * HIST, 8 * HIST), 8 * HIST)
-        v = pre[at, cols]
-        s = sigmoid(v)
-        outer = jnp.broadcast_to(gp[pl.ds(pl.multiple_of(u * 8, 8), 8), cols][:, None, :], (8, HIST, 128))
-        g[at, cols] = (outer.reshape(8 * HIST, 128) * s * (1.0 + v * (1.0 - s))).astype(BF16)
-        return 0
-
-    lax.fori_loop(0, (USERS // 8) * (E // 128), backward, 0)
-    g_copy = send(g, gs, g_s.at[0], g_r.at[0], sibling)
-
-    for copy in loss_copies:
-        copy.wait_recv()
-    loss_copies = reduce_loss(reduced_loss(1), 2, z)
-
-    for copy in x_recv:
-        copy.wait_recv()
-    gi_copy.wait_recv()
-
     pos = (x, y, z)
 
-    def put(k, q, r):
-        r = r.astype(BF16)
-        xh, qz = q // N, lax.rem(q, N)
-        for xl in range(XL):
-            for yy in range(N):
-                at = (xh * XL + xl, yy, qz)
-                i0, i1, i2 = at[k % 3], at[(k + 1) % 3], at[(k + 2) % 3]
-                o = (xl * N + yy) * 16
-                part[k, i0, i1, i2] = r[o:o + 16]
-
-    def own_cols(q):
-        return pl.ds(pl.multiple_of((q * CORES + c) * FEAT, FEAT), FEAT)
-
-    def item_part(q, lo, hi):
-        return dot_t(civ[:, own_cols(q)], gi[:, lo:hi]) + dot_t(cis[q], gis[:, lo:hi])
-
-    def user_part(q, lo, hi):
-        return dot_t(xv[:, own_cols(q)], g[:, lo:hi]) + dot_t(xs[q], gs[:, lo:hi])
-
-    def colour2(q, _):
-        put(2, q, item_part(q, 2 * CW - E, E))
-        return 0
-
-    def colour1(q, _):
-        put(1, q, jnp.concatenate([user_part(q, CW, E), item_part(q, 0, 2 * CW - E)], axis=1))
-        return 0
-
-    def colour0(q, _):
-        put(0, q, user_part(q, 0, CW))
-        return 0
+    def backward(k):
+        def step(n, _):
+            u = n // (CW // 128)
+            j = lax.rem(n, CW // 128)
+            cols = pl.ds(pl.multiple_of(k * CW + j * 128, 128), 128)
+            at = pl.ds(pl.multiple_of(u * 8 * HIST, 8 * HIST), 8 * HIST)
+            v = pre[at, cols]
+            s = sigmoid(v)
+            outer = jnp.broadcast_to(gp[pl.ds(pl.multiple_of(u * 8, 8), 8), cols][:, None, :], (8, HIST, 128))
+            out = (outer.reshape(8 * HIST, 128) * s * (1.0 + v * (1.0 - s))).astype(BF16)
+            g[k, at, pl.ds(pl.multiple_of(j * 128, 128), 128)] = out
+            return 0
+
+        lax.fori_loop(0, (USERS // 8) * (CW // 128), step, 0)
+        return send(g.at[k, pl.ds(0, ROWS)], g.at[k, pl.ds(ROWS, ROWS)], g_s.at[k], g_r.at[k], sibling)
 
     def towards(axis, v):
         at = list(pos)
@@ -350,28 +344,48 @@
             )
         return copies
 
-    lax.fori_loop(0, QN, colour2, 0)
-    flight = {2: phase(2, 0, part, ra)}
+    def weight_grad(k):
+        r = dot(xt[...], g[k]).astype(BF16)
+        for q in range(QN):
+            for xl in range(XL):
+                for yy in range(N):
+                    at = ((q // N) * XL + xl, yy, q % N)
+                    o = (q * XL * N + xl * N + yy) * 16
+                    part[k, at[k % 3], at[(k + 1) % 3], at[(k + 2) % 3]] = r[o:o + 16]
+        return phase(k, 0, part, ra)
+
+    g_copies = [backward(0), backward(1)]
+    g_copies[0].wait_recv()
+    flight = {0: weight_grad(0)}
+    g_copies.append(backward(2))
+    g_copies[1].wait_recv()
+    flight[1] = weight_grad(1)
+    g_copies[2].wait_recv()
+    flight[2] = weight_grad(2)
+
+    for copy in ig_recv:
+        copy.wait_recv()
+    item_grad = pig[0].astype(F32)
+    for n in range(len(item_peers)):
+        item_grad = item_grad + rig[n].astype(F32)
+    ig_ref[...] = item_grad
+    item_normed = inorm[...]
+    radial = jnp.sum(item_normed * item_grad, axis=1, keepdims=True)
+    gi[0] = ((item_grad - item_normed * radial) / ilen[:, 0:1]).astype(BF16)
+    gi_recv = []
+    for n, d in enumerate(feat_peers):
+        gi_recv.append(send(gi.at[0], gi.at[n + 1], gi_s.at[n], gi_r.at[n], feat_peer(*d)))
+
     for copy in loss_copies:
         copy.wait_recv()
-    loss = reduced_loss(2)
-    corelosses[c] = loss
-    core_copy = send(corelosses.at[c], corelosses.at[c], lo_s.at[3, 0], lo_r.at[3, 0], sibling)
-    g_copy.wait_recv()
-    lax.fori_loop(0, QN, colour1, 0)
-    flight[1] = phase(1, 0, part, ra)
-    lax.fori_loop(0, QN, colour0, 0)
-    flight[0] = phase(0, 0, part, ra)
-    core_copy.wait_recv()
-    loss_ref[0] = jnp.sum(corelosses[0] + corelosses[1]) / TOTAL
-
-    order = (2, 1, 0)
-    for k in order:
+    loss_copies = reduce_loss(reduced_loss(0), 1, y)
+
+    def add_a(k):
         for copy in flight[k]:
             copy.wait_recv()
         me = pos[k % 3]
 
-        def add_a(n, _, k=k, me=me):
+        def step(n, _):
             i, j = n // N, lax.rem(n, N)
             total = part[k, me, i, j].astype(F32)
             for d in range(N - 1):
@@ -379,9 +393,10 @@
             sa[k, i, j] = total.astype(BF16)
             return 0
 
-        lax.fori_loop(0, N * N, add_a, 0)
+        lax.fori_loop(0, N * N, step, 0)
         flight[k] = phase(k, 1, sa, rb)
-    for k in order:
+
+    def add_b(k):
         for copy in flight[k]:
             copy.wait_recv()
         me = pos[(k + 1) % 3]
@@ -391,22 +406,64 @@
                 total = total + rb[k, d, j].astype(F32)
             sb[k, j] = total.astype(BF16)
         flight[k] = phase(k, 2, sb, rc)
-    for k in order:
+
+    def add_c(k):
         for copy in flight[k]:
             copy.wait_recv()
-        me = pos[(k + 2) % 3]
-        total = sb[k, me].astype(F32)
+        total = sb[k, pos[(k + 2) % 3]].astype(F32)
         for d in range(N - 1):
             total = total + rc[k, d].astype(F32)
-        if k == 0:
-            gu_ref[:, 0:CW] = total
-        elif k == 1:
-            gu_ref[:, CW:E] = total[:, 0:E - CW]
-            gi_ref[:, 0:2 * CW - E] = total[:, E - CW:CW]
-        else:
-            gi_ref[:, 2 * CW - E:E] = total
+        gu_ref[:, k * CW:(k + 1) * CW] = total
+
+    add_a(0)
+    for copy in loss_copies:
+        copy.wait_recv()
+    loss_copies = reduce_loss(reduced_loss(1), 2, z)
+    add_a(1)
+
+    for copy in xi_recv + gi_recv:
+        copy.wait_recv()
+    for h in range(XH):
+        r = dot_t(
+            xi[h].reshape(N * CORES * USERS, FEAT), gi[...].reshape(N * CORES * USERS, E)
+        ).astype(BF16)
+        for xl in range(XL):
+            for yy in range(N):
+                o = (xl * N + yy) * 16
+                parti[h * XL + xl, yy] = r[o:o + 16]
+    ri_recv = []
+    for n, (dx, dy) in enumerate(row_peers):
+        tx, ty = plus(x, dx, N), plus(y, dy, N)
+        ri_recv.append(send(parti.at[tx, ty], ri.at[n], ri_s.at[n], ri_r.at[n], row_peer(dx, dy)))
+
+    add_a(2)
+    for copy in loss_copies:
+        copy.wait_recv()
+    corelosses[c] = reduced_loss(2)
+    core_copy = send(corelosses.at[c], corelosses.at[c], lo_s.at[3, 0], lo_r.at[3, 0], sibling)
+    add_b(0)
+    add_b(1)
+    add_b(2)
+    core_copy.wait_recv()
+    loss_ref[...] = jnp.broadcast_to(jnp.sum(corelosses[0] + corelosses[1], keepdims=True) / TOTAL, (8, 128))
+    add_c(0)
+    add_c(1)
+    for copy in ri_recv:
+        copy.wait_recv()
+    total = parti[x, y].astype(F32)
+    for n in range(len(row_peers)):
+        total = total + ri[n].astype(F32)
+    gi_ref[...] = total
+    add_c(2)
     for copy in sent:
         copy.wait_send()
+
+
+def hand_out(loss, ig, gu, gi, loss_out, ig_out, gu_out, gi_out):
+    loss_out[0] = loss[0, 0]
+    ig_out[...] = ig[...]
+    gu_out[...] = gu[...]
+    gi_out[...] = gi[...]
 
 
 def shards(N, XL, past, cand, wu, wi, scale, shift, ids, slots):
@@ -419,7 +476,7 @@
     smem = pl.BlockSpec(memory_space=pltpu.SMEM)
     vmem = pl.BlockSpec(memory_space=pltpu.VMEM)
     rows = depth // (NI * N * CORES)
-    CW = 2 * E // COLOURS
+    CW = E // COLOURS
 
     def dma(*shape):
         return pltpu.SemaphoreType.DMA(shape)
@@ -427,7 +484,7 @@
     V = pltpu.VMEM
     scratch = [
         V((users * hist, depth), BF16), V((QN, users * hist, feat), BF16),
-        V((users, depth), BF16), V((QN, users, feat), BF16),
+        V((users, depth), BF16),
         V((depth, E), BF16), V((depth, E), BF16),
         V((users * hist, E), F32), V((users, E), F32), V((users, E), F32), V((users, 128), F32),
         V((users, E), F32), V((users, 128), F32),
@@ -436,27 +493,31 @@
         V((NI * users, NU * users), BF16),
         V((NI, users, E), BF16), V((NI - 1, users, E), BF16),
         V((NU, users, E), BF16), V((NU - 1, users, E), BF16),
-        V((users * hist, E), BF16), V((users * hist, E), BF16), V((users, E), BF16), V((users, E), BF16),
+        V((COLOURS, 2 * users * hist, CW), BF16), V((NU, users, E), BF16),
+        V((N // XL, NU, users, feat), BF16), V((QN * feat, 2 * users * hist), BF16),
         V((COLOURS, N, N, N, rows, CW), BF16), V((COLOURS, N - 1, N, N, rows, CW), BF16),
         V((COLOURS, N, N, rows, CW), BF16), V((COLOURS, N - 1, N, rows, CW), BF16),
         V((COLOURS, N, rows, CW), BF16), V((COLOURS, N - 1, rows, CW), BF16),
+        V((N, N, rows, E), BF16), V((NI - 1, rows, E), BF16),
         V((3, N, 8, 128), F32), V((CORES, 8, 128), F32),
-        dma(4), dma(2 * QN), dma(2 * QN), dma(NI - 1), dma(NI - 1), dma(NU - 1), dma(NU - 1),
+        pltpu.SMEM((1,), F32), pltpu.SMEM((1,), F32), V((1, users), jnp.int32), V((1, users), jnp.int32),
+        dma(8), dma(QN), dma(QN), dma(NU - 1, N // XL), dma(NU - 1, N // XL),
+        dma(NI - 1), dma(NI - 1), dma(NU - 1), dma(NU - 1),
         dma(NU - 1), dma(NU - 1), dma(NI - 1), dma(NI - 1), dma(NU - 1), dma(NU - 1),
-        dma(NI - 1), dma(NI - 1), dma(NU - 1), dma(NU - 1), dma(2), dma(2),
-        dma(COLOURS, 3, N - 1), dma(COLOURS, 3, N - 1), dma(4, N - 1), dma(4, N - 1),
+        dma(NI - 1), dma(NI - 1), dma(NU - 1), dma(NU - 1), dma(COLOURS), dma(COLOURS), dma(NU - 1), dma(NU - 1),
+        dma(COLOURS, 3, N - 1), dma(COLOURS, 3, N - 1), dma(NI - 1), dma(NI - 1), dma(4, N - 1), dma(4, N - 1),
     ]
-    return pl.pallas_call(
+    outs = pl.pallas_call(
         functools.partial(tower_kernel, N, XL, total),
         name="two_tower",
         out_shape=(
-            jax.ShapeDtypeStruct((1,), F32),
+            jax.ShapeDtypeStruct((8, 128), F32),
             jax.ShapeDtypeStruct((users, E), F32),
             jax.ShapeDtypeStruct((rows, E), F32),
             jax.ShapeDtypeStruct((rows, E), F32),
         ),
-        in_specs=[hbm, hbm, hbm, hbm, smem, smem, vmem, vmem],
-        out_specs=(smem, vmem, vmem, vmem),
+        in_specs=[hbm] * 8,
+        out_specs=(vmem,) * 4,
         scratch_shapes=scratch,
         compiler_params=pltpu.CompilerParams(
             collective_id=0, has_side_effects=True, vmem_limit_bytes=60 * 1024 * 1024
@@ -465,6 +526,18 @@
         past.reshape(users * hist, depth), cand, wu, wi, scale, shift,
         ids.reshape(1, users), slots.reshape(1, users),
     )
+    return pl.pallas_call(
+        hand_out,
+        name="hand_out",
+        out_shape=(
+            jax.ShapeDtypeStruct((1,), F32),
+            jax.ShapeDtypeStruct((users, E), F32),
+            jax.ShapeDtypeStruct((rows, E), F32),
+            jax.ShapeDtypeStruct((rows, E), F32),
+        ),
+        in_specs=[vmem] * 4,
+        out_specs=(smem, vmem, vmem, vmem),
+    )(*outs)
 
 
 def solution(mesh):

time: 83.8 us -> 70.5 us (0.84)
  Pallas kernels: 75.4 us -> 67.6 us
  local copies, waits for them, and re-layouts: 4.38 us -> 0 us
  between operations: 3.7 us -> 1.93 us
    pallas_call x1, Pallas kernels: 75.4 us -> 66.1 us  [shards(): pl.pallas_call(functools.partial(tower_kernel, N, XL, total), name='two_t...]
    unnamed x3 -> x0, local copies, waits for them, and re-layouts: 4.38 us -> none
    pallas_call x0 -> x1, Pallas kernels: none -> 1.58 us  [shards(): pl.pallas_call(hand_out, name='hand_out', out_shape=(jax.ShapeDtypeStruct...]
where the time goes in v2:
time: 70.5 us; the launch traced here: 69.6 us
  Pallas kernels  67.6 us (96%)
  between operations  1.93 us (3%)
    pallas_call x1, Pallas kernels, shards(): pl.pallas_call(functools.partial(tower_kernel, N, XL, total), name='two_t...  66.1 us
    pallas_call x1, Pallas kernels, shards(): pl.pallas_call(hand_out, name='hand_out', out_shape=(jax.ShapeDtypeStruct...  1.58 us

profile of v2, /device:TPU:0, one launch (start us, length us, event | category | flops | bytes accessed | tf_op | source)
XLA Modules:
  0.0 69.6 jit_solution(6676959559657033495)
XLA Ops:
  1.9 66.1 %two_tower.1 = (f32[8,128]{1,0:T(8,128)}, f32[32,768]{1,0:T(8,128)}, f32[16,768]{1,0:T(8,128)}, f32[16,768]{1,0:T(8,128)}) custom-call(bf16[768,2048]{1,0:T(8,128)(2,1)} %bitcast.3, bf16[32,2048]{1,0:T(8,128)(2,1)} %ci_hbm.1, bf16[2048,768]{1,0:T(8,128)(2,1)} %wu_hbm.1, bf16[2048,768]{1,0:T(8,128)(2,1)} %wi_hbm.1, f32[1]{0:T(128)S(6)} %copy.12.scale_ref, ...), custom_call_target="tpu_custom_call" | custom-call | tf_op jit(solution)/shard_map/two_tower/pallas_call | solution.py:510
  68.0 1.6 %hand_out.1 = (f32[1]{0:T(128)}, f32[32,768]{1,0:T(8,128)}, f32[16,768]{1,0:T(8,128)}, f32[16,768]{1,0:T(8,128)}) custom-call(f32[8,128]{1,0:T(8,128)} %get-tuple-element.8.loss, f32[32,768]{1,0:T(8,128)} %get-tuple-element.9.ig, f32[16,768]{1,0:T(8,128)} %get-tuple-element.10.gu, f32[16,768]{1,0:T(8,128)} %get-tuple-element.11.gi), custom_call_target="tpu_custom_call" | custom-call | tf_op jit(solution)/shard_map/hand_out/pallas_call | solution.py:529

commit v3 on v2

--- a/solution.py
+++ b/solution.py
@@ -36,18 +36,19 @@
     x_hbm, ci_hbm, wu_hbm, wi_hbm, scale_ref, shift_ref, ids_ref, slot_ref,
     loss_ref, ig_ref, gu_ref, gi_ref,
     xv, xs, civ, wuv, wiv, pre, pooled, gp, ulen, inorm, ilen,
-    ua, ia, idbuf, slotbuf, tgtbuf, wt, pig, rig, pgu, rgu, g, gi, xi, xt,
+    ua, ia, idrow, idbuf, slotbuf, tgtbuf, wt, pig, pigf, rigc, rig, pgu, rgu, g, gi, xi, xt,
     part, ra, sa, rb, sb, rc, parti, ri, losses, corelosses, scale_s, shift_s, idv, slotv,
     lsem, xsem_s, xsem_r, xi_s, xi_r, id_s, id_r, slot_s, slot_r, tgt_s, tgt_r,
     ia_s, ia_r, ua_s, ua_r, ig_s, ig_r, ug_s, ug_r, g_s, g_r, gi_s, gi_r,
-    rs_s, rs_r, ri_s, ri_r, lo_s, lo_r,
+    ra_s, ra_r, rs_s, rs_r, ri_s, ri_r, lo_s, lo_r, hop_s, hop_r,
 ):
     USERS, E = pooled.shape
     HIST = xv.shape[0] // USERS
     FEAT = 128 if N == 4 else XL * N * 16
     QN = (N // XL) * N
-    NU = N * CORES
-    NI = N * N
+    NU = XL * N
+    NI = XL * N * CORES
+    NS = XL * N
     CW = E // COLOURS
     XH = N // XL
     ROWS = USERS * HIST
@@ -57,6 +58,9 @@
     z = lax.rem(blk // CORES, N)
     x = (blk // (CORES * N)) * XL + group // N
     y = lax.rem(group, N)
+    odd = lax.rem(x, 2)
+    pair_a = x + 1 - 2 * odd
+    pair_b = lax.rem(x + N - 1 + 2 * odd, N)
 
     def device(px, py, pz, pc):
         return (((px // XL) * N + pz) * CORES + pc, lax.rem(px, XL) * N + py)
@@ -77,19 +81,26 @@
 
     sent = []
     sibling = device(x, y, z, 1 - c)
-    user_peers = [(dy, dc) for dy in range(N) for dc in range(CORES) if (dy, dc) != (0, 0)]
-    item_peers = [(dx, dz) for dx in range(N) for dz in range(N) if (dx, dz) != (0, 0)]
-    feat_peers = [(dz, dc) for dz in range(N) for dc in range(CORES) if (dz, dc) != (0, 0)]
+    user_peers = [(da, dy) for da in range(2) for dy in range(N) if (da, dy) != (0, 0)]
+    item_peers = [(db, dz, dc) for dc in range(CORES) for db in range(2) for dz in range(N) if (db, dz, dc) != (0, 0, 0)]
+    near_items = [d for d in item_peers if d[2] == 0]
+    feat_peers = [(dz, dc) for dc in range(CORES) for dz in range(N) if (dz, dc) != (0, 0)]
     row_peers = [(dx, dy) for dx in range(N) for dy in range(N) if (dx, dy) != (0, 0)]
 
-    def user_peer(dy, dc):
-        return device(x, plus(y, dy, N), z, plus(c, dc, CORES))
-
-    def user_slot(dy, dc):
-        return plus(y, dy, N) * CORES + plus(c, dc, CORES)
-
-    def item_peer(dx, dz):
-        return device(plus(x, dx, N), y, plus(z, dz, N), c)
+    def user_peer(da, dy):
+        return device(pair_a if da else x, plus(y, dy, N), z, c)
+
+    def user_slot(da, dy):
+        return (1 - odd if da else odd) * N + plus(y, dy, N)
+
+    def item_slot(db, dz, dc):
+        return dc * NS + db * N + dz
+
+    def item_peer(db, dz, dc):
+        return device(pair_b if db else x, y, plus(z, dz, N), plus(c, dc, CORES))
+
+    def item_owner(db, dz, dc):
+        return device(pair_b if db else x, y, minus(z, dz, N), plus(c, dc, CORES))
 
     def feat_peer(dz, dc):
         return device(x, y, plus(z, dz, N), plus(c, dc, CORES))
@@ -111,41 +122,25 @@
         load.start()
 
     barrier = pltpu.get_barrier_semaphore()
-    for d in user_peers:
-        pl.semaphore_signal(barrier, inc=1, device_id=user_peer(*d), device_id_type=MESH)
-    for d in item_peers:
-        pl.semaphore_signal(barrier, inc=1, device_id=item_peer(*d), device_id_type=MESH)
-    far_feat = [d for d in feat_peers if d[0] and d[1]]
-    far_row = [d for d in row_peers if d[0] and d[1]]
-    for d in far_feat:
-        pl.semaphore_signal(barrier, inc=1, device_id=feat_peer(*d), device_id_type=MESH)
-    for d in far_row:
-        pl.semaphore_signal(barrier, inc=1, device_id=row_peer(*d), device_id_type=MESH)
+    greeted = [row_peer(*d) for d in row_peers]
+    greeted += [item_peer(*d) for d in item_peers if (d[1], d[2]) != (0, 0)]
+    for to in greeted:
+        pl.semaphore_signal(barrier, inc=1, device_id=to, device_id_type=MESH)
     for load in small:
         load.wait()
-
+    my_user_slot = user_slot(0, 0)
     rows = lax.broadcasted_iota(jnp.int32, (USERS, USERS), 0)
     lanes = lax.broadcasted_iota(jnp.int32, (USERS, USERS), 1)
     id_col = jnp.sum(jnp.where(rows == lanes, idv[...].astype(F32), 0.0), axis=1, keepdims=True)
     slot_col = jnp.sum(jnp.where(rows == lanes, slotv[...].astype(F32), 0.0), axis=1, keepdims=True)
-    idbuf[0] = jnp.broadcast_to(id_col, (USERS, 128))
-    my_user_slot = y * CORES + c
+    tile_rows = lax.broadcasted_iota(jnp.int32, (USERS, 128), 0)
+    tile_lanes = lax.broadcasted_iota(jnp.int32, (USERS, 128), 1)
+    idrow[0] = jnp.sum(jnp.where(tile_rows == tile_lanes, id_col, 0.0), axis=0, keepdims=True)
     wide_rows = lax.broadcasted_iota(jnp.int32, (USERS, NU * USERS), 0)
     wide_lanes = lax.broadcasted_iota(jnp.int32, (USERS, NU * USERS), 1)
-    slot_row = jnp.sum(
+    slotbuf[0] = jnp.sum(
         jnp.where(wide_lanes == wide_rows + my_user_slot * USERS, slot_col, 0.0), axis=0, keepdims=True
     )
-    slotbuf[0] = jnp.broadcast_to(slot_row, (8, NU * USERS))
-
-    pl.semaphore_wait(barrier, len(user_peers) + len(item_peers) + len(far_feat) + len(far_row))
-
-    id_recv, slot_recv = [], []
-    for n, d in enumerate(user_peers):
-        slot_recv.append(send(slotbuf.at[0], slotbuf.at[n + 1], slot_s.at[n], slot_r.at[n], user_peer(*d)))
-    for n, (dx, dz) in enumerate(item_peers):
-        s = dx * N + dz
-        id_recv.append(send(idbuf.at[0], idbuf.at[s], id_s.at[n], id_r.at[n], item_peer(dx, dz)))
-
     load_ci.wait()
     load_wi.wait()
     item_pre = dot(civ[...], wiv[...])
@@ -153,25 +148,21 @@
     item_normed = item_pre / item_len
     inorm[...] = item_normed
     ilen[...] = jnp.broadcast_to(item_len, (USERS, 128))
-    ia[0] = item_normed.astype(BF16)
+    ia[0, 0] = item_normed.astype(BF16)
+    pl.semaphore_wait(barrier, len(greeted))
+    id_recv, slot_recv = [], []
+    for n, d in enumerate(user_peers):
+        slot_recv.append(send(slotbuf.at[0], slotbuf.at[n + 1], slot_s.at[n], slot_r.at[n], user_peer(*d)))
+    for n, d in enumerate(item_peers):
+        id_recv.append(send(idrow.at[0], idrow.at[item_slot(*d)], id_s.at[n], id_r.at[n], item_peer(*d)))
     ia_recv = []
-    for n, (dx, dz) in enumerate(item_peers):
-        s = dx * N + dz
-        ia_recv.append(send(ia.at[0], ia.at[s], ia_s.at[n], ia_r.at[n], item_peer(dx, dz)))
-
+    for n, d in enumerate(near_items):
+        ia_recv.append(send(ia.at[0, 0], ia.at[0, item_slot(*d)], ia_s.at[n], ia_r.at[n], item_peer(*d)))
     load_x.wait()
     x_recv = []
     for q in range(QN):
         cols = pl.ds(pl.multiple_of((q * CORES + 1 - c) * FEAT, FEAT), FEAT)
         x_recv.append(send(xv.at[:, cols], xs.at[q], xsem_s.at[q], xsem_r.at[q], sibling))
-    xi_recv = []
-    for n, (dz, dc) in enumerate(feat_peers):
-        pz, pc = plus(z, dz, N), plus(c, dc, CORES)
-        for h in range(XH):
-            cols = pl.ds(pl.multiple_of(((h * N + pz) * CORES + pc) * FEAT, FEAT), FEAT)
-            xi_recv.append(
-                send(civ.at[:, cols], xi.at[h, n + 1], xi_s.at[n, h], xi_r.at[n, h], feat_peer(dz, dc))
-            )
     load_wu.wait()
 
     def forward(n, _):
@@ -180,6 +171,31 @@
         return 0
 
     lax.fori_loop(0, E // 256, forward, 0)
+
+    for copy in slot_recv + id_recv:
+        copy.wait_recv()
+    slots = slotbuf[0]
+    for n in range(1, NU):
+        slots = slots + slotbuf[n]
+    wide = NU * USERS // 128
+    found = jnp.zeros((1, NU * USERS), F32)
+    for dc in range(CORES):
+        for db in range(2):
+            for dz in range(N):
+                s = item_slot(db, dz, dc)
+                col = jnp.sum(jnp.where(tile_rows == tile_lanes, idrow[s], 0.0), axis=1, keepdims=True)
+                ids = jnp.broadcast_to(col, (USERS, 128))
+                idbuf[s] = ids
+                ob, og = item_owner(db, dz, dc)
+                at = (tile_rows + (ob * (XL * N) + og) * USERS).astype(F32)
+                hit = jnp.concatenate([at] * wide, axis=1) == slots
+                found = found + jnp.sum(
+                    jnp.where(hit, jnp.concatenate([ids] * wide, axis=1), 0.0), axis=0, keepdims=True
+                )
+    tgtbuf[0] = found
+    tgt_recv = []
+    for n, d in enumerate(user_peers):
+        tgt_recv.append(send(tgtbuf.at[0], tgtbuf.at[n + 1], tgt_s.at[n], tgt_r.at[n], user_peer(*d)))
 
     def pool(n, _):
         u = n // (E // 128)
@@ -201,8 +217,19 @@
     for n, d in enumerate(user_peers):
         ua_recv.append(send(ua.at[my_user_slot], ua.at[my_user_slot], ua_s.at[n], ua_r.at[n], user_peer(*d)))
 
+    xi_recv = []
+    for n, (dz, dc) in enumerate(feat_peers):
+        pz, pc = plus(z, dz, N), plus(c, dc, CORES)
+        for h in range(XH):
+            cols = pl.ds(pl.multiple_of(((h * N + pz) * CORES + pc) * FEAT, FEAT), FEAT)
+            xi_recv.append(
+                send(civ.at[:, cols], xi.at[h, dc * N + dz], xi_s.at[n, h], xi_r.at[n, h], feat_peer(dz, dc))
+            )
     for h in range(XH):
         xi[h, 0] = civ[:, pl.ds(pl.multiple_of(((h * N + z) * CORES + c) * FEAT, FEAT), FEAT)]
+    for copy in ia_recv:
+        copy.wait_recv()
+    ia_hop = send(ia.at[0], ia.at[1], hop_s.at[0], hop_r.at[0], sibling)
     for copy in x_recv:
         copy.wait_recv()
 
@@ -214,74 +241,32 @@
         return 0
 
     lax.fori_loop(0, QN, turn, 0)
-    for copy in slot_recv + id_recv:
-        copy.wait_recv()
-    slots = slotbuf[0]
-    for n in range(1, NU):
-        slots = slots + slotbuf[n]
-    slots = slots[0:1]
-    found = jnp.zeros((1, NU * USERS), F32)
-    item_rows = lax.broadcasted_iota(jnp.int32, (USERS, 128), 0)
-    for dx in range(N):
-        for dz in range(N):
-            ox, oz = minus(x, dx, N), minus(z, dz, N)
-            ob, og = device(ox, y, oz, c)
-            at = (item_rows + (ob * (XL * N) + og) * USERS).astype(F32)
-            ids = idbuf[dx * N + dz]
-            wide = NU * USERS // 128
-            hit = jnp.concatenate([at] * wide, axis=1) == slots
-            found = found + jnp.sum(
-                jnp.where(hit, jnp.concatenate([ids] * wide, axis=1), 0.0), axis=0, keepdims=True
-            )
-    tgtbuf[0] = jnp.broadcast_to(found, (8, NU * USERS))
-    tgt_recv = []
-    for n, d in enumerate(user_peers):
-        tgt_recv.append(send(tgtbuf.at[0], tgtbuf.at[n + 1], tgt_s.at[n], tgt_r.at[n], user_peer(*d)))
     for copy in tgt_recv:
         copy.wait_recv()
     targets = tgtbuf[0]
     for n in range(1, NU):
         targets = targets + tgtbuf[n]
-    targets = targets[0:1]
-
-    for copy in ua_recv + ia_recv:
-        copy.wait_recv()
+
+    for copy in ua_recv:
+        copy.wait_recv()
+    ia_hop.wait_recv()
     scale = scale_s[0]
     shift = shift_s[0]
     users = ua[...].reshape(NU * USERS, E)
     loss = jnp.zeros((8, 128), F32)
-    wide = NU * USERS // 128
-    for dx in range(N):
-        items = ia[dx * N:(dx + 1) * N].reshape(N * USERS, E)
+    for n in range(NI // N):
+        items = ia[n // 2, (n % 2) * N:(n % 2 + 1) * N].reshape(N * USERS, E)
         scores = dot_nt(items, users)
-        ids = idbuf[dx * N:(dx + 1) * N].reshape(N * USERS, 128)
+        ids = idbuf[n * N:(n + 1) * N].reshape(N * USERS, 128)
         sign = jnp.where(jnp.concatenate([ids] * wide, axis=1) == targets, 1.0, -1.0)
         margin = sign * (scale * scores + shift)
         e = jnp.exp(-jnp.abs(margin))
         terms = jnp.log1p(e) + jnp.maximum(-margin, 0.0)
         gate = jnp.where(margin >= 0.0, e, 1.0) / (1.0 + e)
-        wt[dx * N * USERS:(dx + 1) * N * USERS, :] = (-scale * sign * gate).astype(BF16)
+        wt[n * N * USERS:(n + 1) * N * USERS, :] = (-scale * sign * gate).astype(BF16)
         terms = jnp.sum(terms.reshape(N * USERS // 8, 8, NU * USERS), axis=0)
         for j in range(wide):
             loss = loss + terms[:, j * 128:(j + 1) * 128]
-    pgu[...] = dot_t(wt[...], ia[...].reshape(NI * USERS, E)).astype(BF16).reshape(NU, USERS, E)
-    ug_recv = []
-    for n, (dy, dc) in enumerate(user_peers):
-        s = user_slot(dy, dc)
-        ug_recv.append(send(pgu.at[s], rgu.at[n], ug_s.at[n], ug_r.at[n], user_peer(dy, dc)))
-    ig_recv = []
-    peer_at = {d: n for n, d in enumerate(item_peers)}
-    for dx in range(N):
-        pig[dx * N:(dx + 1) * N] = (
-            dot(wt[dx * N * USERS:(dx + 1) * N * USERS, :], users).astype(BF16).reshape(N, USERS, E)
-        )
-        for dz in range(N):
-            if (dx, dz) == (0, 0):
-                continue
-            n = peer_at[(dx, dz)]
-            to = device(minus(x, dx, N), y, minus(z, dz, N), c)
-            ig_recv.append(send(pig.at[dx * N + dz], rig.at[n], ig_s.at[n], ig_r.at[n], to))
-
     def reduce_loss(value, step, pos):
         losses[step, pos] = value
         copies = []
@@ -301,6 +286,21 @@
         return total
 
     loss_copies = reduce_loss(loss, 0, x)
+    pgu[...] = dot_t(wt[...], ia[...].reshape(NI * USERS, E)).astype(BF16).reshape(NU, USERS, E)
+    ug_recv = []
+    for n, d in enumerate(user_peers):
+        ug_recv.append(send(pgu.at[user_slot(*d)], rgu.at[n], ug_s.at[n], ug_r.at[n], user_peer(*d)))
+    pig[1] = dot(wt[NS * USERS:2 * NS * USERS, :], users).astype(BF16).reshape(NS, USERS, E)
+    ig_hop = send(pig.at[1], rigc, hop_s.at[1], hop_r.at[1], sibling)
+    pigf[...] = dot(wt[0:NS * USERS, :], users).reshape(NS, USERS, E)
+    ig_hop.wait_recv()
+    ig_recv = []
+    for s in range(NS):
+        pigf[s] = pigf[s] + rigc[s].astype(F32)
+        if s > 0:
+            pig[0, s] = pigf[s].astype(BF16)
+    for n, d in enumerate(near_items):
+        ig_recv.append(send(pig.at[0, item_slot(*d)], rig.at[n], ig_s.at[n], ig_r.at[n], item_owner(*d)))
 
     for copy in ug_recv:
         copy.wait_recv()
@@ -339,50 +339,86 @@
         copies = []
         for d in range(1, N):
             t = plus(pos[axis], d, N)
-            copies.append(
-                send(src.at[k, t], dst.at[k, d - 1], rs_s.at[k, ph, d - 1], rs_r.at[k, ph, d - 1], towards(axis, t))
-            )
+            at = (k, ph - 1, d - 1)
+            copies.append(send(src.at[k, t], dst.at[k, d - 1], rs_s.at[at], rs_r.at[at], towards(axis, t)))
         return copies
 
-    def weight_grad(k):
-        r = dot(xt[...], g[k]).astype(BF16)
-        for q in range(QN):
+    def weight_grad(half, k):
+        xh = x // XL if half else XH - 1 - x // XL
+        depth = QN // XH * FEAT
+        r = dot(xt[pl.ds(pl.multiple_of(xh * depth, depth), depth)], g[k]).astype(BF16)
+        for qz in range(N):
             for xl in range(XL):
                 for yy in range(N):
-                    at = ((q // N) * XL + xl, yy, q % N)
-                    o = (q * XL * N + xl * N + yy) * 16
+                    at = (xh * XL + xl, yy, qz)
+                    o = ((qz * XL + xl) * N + yy) * 16
                     part[k, at[k % 3], at[(k + 1) % 3], at[(k + 2) % 3]] = r[o:o + 16]
-        return phase(k, 0, part, ra)
+        xs_here = pl.ds(xh * XL, XL)
+        if k == 0:
+            for t in ([pair_a] if half else [xh * XL + xl for xl in range(XL)]):
+                d = lax.rem(t - x + N, N) - 1
+                send(part.at[0, t], ra.at[0, d], ra_s.at[0, d, 0], ra_r.at[0, d, 0], towards(0, t))
+            return
+        for d in range(1, N):
+            t = plus(pos[k], d, N)
+            if k == 1:
+                src, dst = part.at[1, t, :, xs_here], ra.at[1, d - 1, :, xs_here]
+            else:
+                src, dst = part.at[2, t, xs_here], ra.at[2, d - 1, xs_here]
+            send(src, dst, ra_s.at[k, d - 1, half], ra_r.at[k, d - 1, half], towards(k, t))
+
+    def wait_slabs(k):
+        for d in range(N - 1):
+            if k == 0:
+                slabs = [ra.at[0, d]]
+            elif k == 1:
+                slabs = [ra.at[1, d, :, pl.ds(h * XL, XL)] for h in range(XH)]
+            else:
+                slabs = [ra.at[2, d, pl.ds(h * XL, XL)] for h in range(XH)]
+            for h, slab in enumerate(slabs):
+                pltpu.make_async_remote_copy(
+                    src_ref=slab, dst_ref=slab, send_sem=ra_s.at[k, d, h], recv_sem=ra_r.at[k, d, h],
+                    device_id=sibling, device_id_type=MESH,
+                ).wait_recv()
 
     g_copies = [backward(0), backward(1)]
+    for copy in loss_copies:
+        copy.wait_recv()
+    loss_copies = reduce_loss(reduced_loss(0), 1, y)
     g_copies[0].wait_recv()
-    flight = {0: weight_grad(0)}
+    weight_grad(0, 0)
     g_copies.append(backward(2))
     g_copies[1].wait_recv()
-    flight[1] = weight_grad(1)
+    weight_grad(0, 1)
     g_copies[2].wait_recv()
-    flight[2] = weight_grad(2)
+    weight_grad(0, 2)
 
     for copy in ig_recv:
         copy.wait_recv()
-    item_grad = pig[0].astype(F32)
-    for n in range(len(item_peers)):
+    item_grad = pigf[0]
+    for n in range(len(near_items)):
         item_grad = item_grad + rig[n].astype(F32)
     ig_ref[...] = item_grad
     item_normed = inorm[...]
     radial = jnp.sum(item_normed * item_grad, axis=1, keepdims=True)
-    gi[0] = ((item_grad - item_normed * radial) / ilen[:, 0:1]).astype(BF16)
+    gi[0, 0] = ((item_grad - item_normed * radial) / ilen[:, 0:1]).astype(BF16)
     gi_recv = []
-    for n, d in enumerate(feat_peers):
-        gi_recv.append(send(gi.at[0], gi.at[n + 1], gi_s.at[n], gi_r.at[n], feat_peer(*d)))
-
+    for d in range(1, N):
+        to = device(x, y, plus(z, d, N), c)
+        gi_recv.append(send(gi.at[0, 0], gi.at[0, d], gi_s.at[d - 1], gi_r.at[d - 1], to))
+    for k in range(COLOURS):
+        weight_grad(1, k)
     for copy in loss_copies:
         copy.wait_recv()
-    loss_copies = reduce_loss(reduced_loss(0), 1, y)
+    loss_copies = reduce_loss(reduced_loss(1), 2, z)
+    for copy in gi_recv:
+        copy.wait_recv()
+    gi_hop = send(gi.at[0], gi.at[1], hop_s.at[2], hop_r.at[2], sibling)
+
+    flight = {}
 
     def add_a(k):
-        for copy in flight[k]:
-            copy.wait_recv()
+        wait_slabs(k)
         me = pos[k % 3]
 
         def step(n, _):
@@ -416,13 +452,15 @@
         gu_ref[:, k * CW:(k + 1) * CW] = total
 
     add_a(0)
+    add_a(1)
+    add_a(2)
     for copy in loss_copies:
         copy.wait_recv()
-    loss_copies = reduce_loss(reduced_loss(1), 2, z)
-    add_a(1)
-
-    for copy in xi_recv + gi_recv:
-        copy.wait_recv()
+    corelosses[c] = reduced_loss(2)
+    core_copy = send(corelosses.at[c], corelosses.at[c], hop_s.at[3], hop_r.at[3], sibling)
+    for copy in xi_recv:
+        copy.wait_recv()
+    gi_hop.wait_recv()
     for h in range(XH):
         r = dot_t(
             xi[h].reshape(N * CORES * USERS, FEAT), gi[...].reshape(N * CORES * USERS, E)
@@ -435,12 +473,6 @@
     for n, (dx, dy) in enumerate(row_peers):
         tx, ty = plus(x, dx, N), plus(y, dy, N)
         ri_recv.append(send(parti.at[tx, ty], ri.at[n], ri_s.at[n], ri_r.at[n], row_peer(dx, dy)))
-
-    add_a(2)
-    for copy in loss_copies:
-        copy.wait_recv()
-    corelosses[c] = reduced_loss(2)
-    core_copy = send(corelosses.at[c], corelosses.at[c], lo_s.at[3, 0], lo_r.at[3, 0], sibling)
     add_b(0)
     add_b(1)
     add_b(2)
@@ -470,12 +502,12 @@
     users, hist, depth = past.shape
     E = wu.shape[1]
     total = users * lax.axis_size("blk") * lax.axis_size("group")
-    NU, NI, QN = N * CORES, N * N, (N // XL) * N
+    NU, NI, NS, QN = XL * N, XL * N * CORES, XL * N, (N // XL) * N
     feat = depth // (QN * CORES)
     hbm = pl.BlockSpec(memory_space=pl.ANY)
     smem = pl.BlockSpec(memory_space=pltpu.SMEM)
     vmem = pl.BlockSpec(memory_space=pltpu.VMEM)
-    rows = depth // (NI * N * CORES)
+    rows = depth // (N * N * N * CORES)
     CW = E // COLOURS
 
     def dma(*shape):
@@ -488,24 +520,26 @@
         V((depth, E), BF16), V((depth, E), BF16),
         V((users * hist, E), F32), V((users, E), F32), V((users, E), F32), V((users, 128), F32),
         V((users, E), F32), V((users, 128), F32),
-        V((NU, users, E), BF16), V((NI, users, E), BF16), V((NI, users, 128), F32),
-        V((NU, 8, NU * users), F32), V((NU, 8, NU * users), F32),
+        V((NU, users, E), BF16), V((CORES, NS, users, E), BF16), V((NI, 1, 128), F32), V((NI, users, 128), F32),
+        V((NU, 1, NU * users), F32), V((NU, 1, NU * users), F32),
         V((NI * users, NU * users), BF16),
-        V((NI, users, E), BF16), V((NI - 1, users, E), BF16),
+        V((CORES, NS, users, E), BF16), V((NS, users, E), F32), V((NS, users, E), BF16),
+        V((NS - 1, users, E), BF16),
         V((NU, users, E), BF16), V((NU - 1, users, E), BF16),
-        V((COLOURS, 2 * users * hist, CW), BF16), V((NU, users, E), BF16),
-        V((N // XL, NU, users, feat), BF16), V((QN * feat, 2 * users * hist), BF16),
+        V((COLOURS, 2 * users * hist, CW), BF16), V((CORES, N, users, E), BF16),
+        V((N // XL, N * CORES, users, feat), BF16), V((QN * feat, 2 * users * hist), BF16),
         V((COLOURS, N, N, N, rows, CW), BF16), V((COLOURS, N - 1, N, N, rows, CW), BF16),
         V((COLOURS, N, N, rows, CW), BF16), V((COLOURS, N - 1, N, rows, CW), BF16),
         V((COLOURS, N, rows, CW), BF16), V((COLOURS, N - 1, rows, CW), BF16),
-        V((N, N, rows, E), BF16), V((NI - 1, rows, E), BF16),
+        V((N, N, rows, E), BF16), V((N * N - 1, rows, E), BF16),
         V((3, N, 8, 128), F32), V((CORES, 8, 128), F32),
         pltpu.SMEM((1,), F32), pltpu.SMEM((1,), F32), V((1, users), jnp.int32), V((1, users), jnp.int32),
-        dma(8), dma(QN), dma(QN), dma(NU - 1, N // XL), dma(NU - 1, N // XL),
-        dma(NI - 1), dma(NI - 1), dma(NU - 1), dma(NU - 1),
-        dma(NU - 1), dma(NU - 1), dma(NI - 1), dma(NI - 1), dma(NU - 1), dma(NU - 1),
-        dma(NI - 1), dma(NI - 1), dma(NU - 1), dma(NU - 1), dma(COLOURS), dma(COLOURS), dma(NU - 1), dma(NU - 1),
-        dma(COLOURS, 3, N - 1), dma(COLOURS, 3, N - 1), dma(NI - 1), dma(NI - 1), dma(4, N - 1), dma(4, N - 1),
+        dma(8), dma(QN), dma(QN), dma(N * CORES - 1, N // XL), dma(N * CORES - 1, N // XL),
+        dma(NI - 1), dma(NI - 1), dma(NU - 1), dma(NU - 1), dma(NU - 1), dma(NU - 1),
+        dma(NS - 1), dma(NS - 1), dma(NU - 1), dma(NU - 1),
+        dma(NS - 1), dma(NS - 1), dma(NU - 1), dma(NU - 1), dma(COLOURS), dma(COLOURS), dma(N - 1), dma(N - 1),
+        dma(COLOURS, N - 1, 2), dma(COLOURS, N - 1, 2), dma(COLOURS, 2, N - 1), dma(COLOURS, 2, N - 1),
+        dma(N * N - 1), dma(N * N - 1), dma(3, N - 1), dma(3, N - 1), dma(4), dma(4),
     ]
     outs = pl.pallas_call(
         functools.partial(tower_kernel, N, XL, total),

time: 70.5 us -> 61.8 us (0.88); the launches traced: 69.6 us -> 61.6 us
  Pallas kernels: 67.6 us -> 59.7 us
    pallas_call x1, Pallas kernels: 66.1 us -> 58.1 us  [shards(): pl.pallas_call(functools.partial(tower_kernel, N, XL, total), name='two_t...]
where the time goes in v3:
time: 61.8 us; the launch traced here: 61.6 us
  Pallas kernels  59.7 us (97%)
  between operations  1.93 us (3%)
    pallas_call x1, Pallas kernels, shards(): pl.pallas_call(functools.partial(tower_kernel, N, XL, total), name='two_t...  58.1 us
    pallas_call x1, Pallas kernels, shards(): pl.pallas_call(hand_out, name='hand_out', out_shape=(jax.ShapeDtypeStruct...  1.58 us

profile of v3, /device:TPU:0, one launch (start us, length us, event | category | flops | bytes accessed | tf_op | source)
XLA Modules:
  0.0 61.6 jit_solution(14256267810736972669)
XLA Ops:
  1.9 58.1 %two_tower.1 = (f32[8,128]{1,0:T(8,128)}, f32[32,768]{1,0:T(8,128)}, f32[16,768]{1,0:T(8,128)}, f32[16,768]{1,0:T(8,128)}) custom-call(bf16[768,2048]{1,0:T(8,128)(2,1)} %bitcast.3, bf16[32,2048]{1,0:T(8,128)(2,1)} %ci_hbm.1, bf16[2048,768]{1,0:T(8,128)(2,1)} %wu_hbm.1, bf16[2048,768]{1,0:T(8,128)(2,1)} %wi_hbm.1, f32[1]{0:T(128)S(6)} %copy.12.scale_ref, ...), custom_call_target="tpu_custom_call" | custom-call | tf_op jit(solution)/shard_map/two_tower/pallas_call | solution.py:544
  60.1 1.6 %hand_out.1 = (f32[1]{0:T(128)}, f32[32,768]{1,0:T(8,128)}, f32[16,768]{1,0:T(8,128)}, f32[16,768]{1,0:T(8,128)}) custom-call(f32[8,128]{1,0:T(8,128)} %get-tuple-element.8.loss, f32[32,768]{1,0:T(8,128)} %get-tuple-element.9.ig, f32[16,768]{1,0:T(8,128)} %get-tuple-element.10.gu, f32[16,768]{1,0:T(8,128)} %get-tuple-element.11.gi), custom_call_target="tpu_custom_call" | custom-call | tf_op jit(solution)/shard_map/hand_out/pallas_call | solution.py:563

commit v4 on v3

--- a/solution.py
+++ b/solution.py
@@ -13,6 +13,7 @@
 BF16 = jnp.bfloat16
 CORES = 2
 COLOURS = 3
+HOME = 2
 
 
 def dot(a, b):
@@ -37,7 +38,7 @@
     loss_ref, ig_ref, gu_ref, gi_ref,
     xv, xs, civ, wuv, wiv, pre, pooled, gp, ulen, inorm, ilen,
     ua, ia, idrow, idbuf, slotbuf, tgtbuf, wt, pig, pigf, rigc, rig, pgu, rgu, g, gi, xi, xt,
-    part, ra, sa, rb, sb, rc, parti, ri, losses, corelosses, scale_s, shift_s, idv, slotv,
+    part, ra0, ra1, ra2, sa, rb, parti, ri, losses, corelosses, scale_s, shift_s, idv, slotv,
     lsem, xsem_s, xsem_r, xi_s, xi_r, id_s, id_r, slot_s, slot_r, tgt_s, tgt_r,
     ia_s, ia_r, ua_s, ua_r, ig_s, ig_r, ug_s, ug_r, g_s, g_r, gi_s, gi_r,
     ra_s, ra_r, rs_s, rs_r, ri_s, ri_r, lo_s, lo_r, hop_s, hop_r,
@@ -79,13 +80,30 @@
         sent.append(copy)
         return copy
 
+    def arrived(dst, sem):
+        pltpu.make_async_remote_copy(
+            src_ref=dst, dst_ref=dst, send_sem=sem, recv_sem=sem, device_id=sibling, device_id_type=MESH
+        ).wait_recv()
+
+    def left(src, sem):
+        pltpu.make_async_remote_copy(
+            src_ref=src, dst_ref=src, send_sem=sem, recv_sem=sem, device_id=sibling, device_id_type=MESH
+        ).wait_send()
+
     sent = []
     sibling = device(x, y, z, 1 - c)
-    user_peers = [(da, dy) for da in range(2) for dy in range(N) if (da, dy) != (0, 0)]
-    item_peers = [(db, dz, dc) for dc in range(CORES) for db in range(2) for dz in range(N) if (db, dz, dc) != (0, 0, 0)]
-    near_items = [d for d in item_peers if d[2] == 0]
-    feat_peers = [(dz, dc) for dc in range(CORES) for dz in range(N) if (dz, dc) != (0, 0)]
-    row_peers = [(dx, dy) for dx in range(N) for dy in range(N) if (dx, dy) != (0, 0)]
+    def ring(d):
+        return min(d, N - d)
+
+    span = range(N)
+    user_peers = [(da, dy) for da in range(2) for dy in span if (da, dy) != (0, 0)]
+    user_peers.sort(key=lambda p: -p[0] - ring(p[1]))
+    near_items = [(db, dz, 0) for db in range(2) for dz in span if (db, dz) != (0, 0)]
+    near_items.sort(key=lambda p: -p[0] - ring(p[1]))
+    item_peers = near_items + [(db, dz, 1) for db in range(2) for dz in span]
+    planes = [(di, dj) for di in span for dj in span if (di, dj) != (0, 0)]
+    planes.sort(key=lambda p: -ring(p[0]) - ring(p[1]))
+    steps = sorted(range(1, N), key=lambda d: -ring(d))
 
     def user_peer(da, dy):
         return device(pair_a if da else x, plus(y, dy, N), z, c)
@@ -101,9 +119,6 @@
 
     def item_owner(db, dz, dc):
         return device(pair_b if db else x, y, minus(z, dz, N), plus(c, dc, CORES))
-
-    def feat_peer(dz, dc):
-        return device(x, y, plus(z, dz, N), plus(c, dc, CORES))
 
     def row_peer(dx, dy):
         return device(plus(x, dx, N), plus(y, dy, N), z, c)
@@ -122,8 +137,10 @@
         load.start()
 
     barrier = pltpu.get_barrier_semaphore()
-    greeted = [row_peer(*d) for d in row_peers]
-    greeted += [item_peer(*d) for d in item_peers if (d[1], d[2]) != (0, 0)]
+    greeted = [row_peer(*d) for d in planes]
+    greeted += [device(plus(x, dx, N), y, plus(z, dz, N), c) for dx in range(N) for dz in range(1, N)]
+    greeted += [device(x, plus(y, dy, N), plus(z, dz, N), c) for dy in range(1, N) for dz in range(1, N)]
+    greeted += [item_peer(*d) for d in item_peers if d[2]]
     for to in greeted:
         pl.semaphore_signal(barrier, inc=1, device_id=to, device_id_type=MESH)
     for load in small:
@@ -198,15 +215,14 @@
         tgt_recv.append(send(tgtbuf.at[0], tgtbuf.at[n + 1], tgt_s.at[n], tgt_r.at[n], user_peer(*d)))
 
     def pool(n, _):
-        u = n // (E // 128)
-        j = lax.rem(n, E // 128)
-        cols = pl.ds(pl.multiple_of(j * 128, 128), 128)
+        u = n // COLOURS
+        cols = pl.ds(pl.multiple_of(lax.rem(n, COLOURS) * CW, CW), CW)
         v = pre[pl.ds(pl.multiple_of(u * 8 * HIST, 8 * HIST), 8 * HIST), cols]
         act = v * sigmoid(v)
-        pooled[pl.ds(pl.multiple_of(u * 8, 8), 8), cols] = jnp.sum(act.reshape(8, HIST, 128), axis=1) / HIST
+        pooled[pl.ds(pl.multiple_of(u * 8, 8), 8), cols] = jnp.sum(act.reshape(8, HIST, CW), axis=1) / HIST
         return 0
 
-    lax.fori_loop(0, (USERS // 8) * (E // 128), pool, 0)
+    lax.fori_loop(0, (USERS // 8) * COLOURS, pool, 0)
     mean = pooled[...]
     user_len = jnp.sqrt(jnp.sum(mean * mean, axis=1, keepdims=True) + EPS)
     user_normed = mean / user_len
@@ -218,15 +234,13 @@
         ua_recv.append(send(ua.at[my_user_slot], ua.at[my_user_slot], ua_s.at[n], ua_r.at[n], user_peer(*d)))
 
     xi_recv = []
-    for n, (dz, dc) in enumerate(feat_peers):
-        pz, pc = plus(z, dz, N), plus(c, dc, CORES)
-        for h in range(XH):
-            cols = pl.ds(pl.multiple_of(((h * N + pz) * CORES + pc) * FEAT, FEAT), FEAT)
-            xi_recv.append(
-                send(civ.at[:, cols], xi.at[h, dc * N + dz], xi_s.at[n, h], xi_r.at[n, h], feat_peer(dz, dc))
-            )
-    for h in range(XH):
-        xi[h, 0] = civ[:, pl.ds(pl.multiple_of(((h * N + z) * CORES + c) * FEAT, FEAT), FEAT)]
+    for n, (db, dz, dc) in enumerate(item_peers):
+        px, pz, pc = pair_b if db else x, plus(z, dz, N), plus(c, dc, CORES)
+        cols = pl.ds(pl.multiple_of(((px // XL * N + pz) * CORES + pc) * FEAT, FEAT), FEAT)
+        xi_recv.append(
+            send(civ.at[:, cols], xi.at[item_slot(db, dz, dc)], xi_s.at[n], xi_r.at[n], item_peer(db, dz, dc))
+        )
+    xi[0] = civ[:, pl.ds(pl.multiple_of(((x // XL * N + z) * CORES + c) * FEAT, FEAT), FEAT)]
     for copy in ia_recv:
         copy.wait_recv()
     ia_hop = send(ia.at[0], ia.at[1], hop_s.at[0], hop_r.at[0], sibling)
@@ -313,182 +327,177 @@
 
     pos = (x, y, z)
 
-    def backward(k):
-        def step(n, _):
-            u = n // (CW // 128)
-            j = lax.rem(n, CW // 128)
-            cols = pl.ds(pl.multiple_of(k * CW + j * 128, 128), 128)
+    def backward(k, _):
+        cols = pl.ds(pl.multiple_of(k * CW, CW), CW)
+
+        def step(u, _):
             at = pl.ds(pl.multiple_of(u * 8 * HIST, 8 * HIST), 8 * HIST)
             v = pre[at, cols]
             s = sigmoid(v)
-            outer = jnp.broadcast_to(gp[pl.ds(pl.multiple_of(u * 8, 8), 8), cols][:, None, :], (8, HIST, 128))
-            out = (outer.reshape(8 * HIST, 128) * s * (1.0 + v * (1.0 - s))).astype(BF16)
-            g[k, at, pl.ds(pl.multiple_of(j * 128, 128), 128)] = out
+            outer = jnp.broadcast_to(gp[pl.ds(pl.multiple_of(u * 8, 8), 8), cols][:, None, :], (8, HIST, CW))
+            g[k, at] = (outer.reshape(8 * HIST, CW) * s * (1.0 + v * (1.0 - s))).astype(BF16)
             return 0
 
-        lax.fori_loop(0, (USERS // 8) * (CW // 128), step, 0)
-        return send(g.at[k, pl.ds(0, ROWS)], g.at[k, pl.ds(ROWS, ROWS)], g_s.at[k], g_r.at[k], sibling)
+        lax.fori_loop(0, USERS // 8, step, 0)
+        pltpu.make_async_remote_copy(
+            src_ref=g.at[k, pl.ds(0, ROWS)], dst_ref=g.at[k, pl.ds(ROWS, ROWS)], send_sem=g_s.at[k],
+            recv_sem=g_r.at[k], device_id=sibling, device_id_type=MESH,
+        ).start()
+        return 0
 
     def towards(axis, v):
         at = list(pos)
         at[axis] = v
         return device(at[0], at[1], at[2], c)
 
-    def phase(k, ph, src, dst):
-        axis = (k + ph) % 3
-        copies = []
-        for d in range(1, N):
-            t = plus(pos[axis], d, N)
-            at = (k, ph - 1, d - 1)
-            copies.append(send(src.at[k, t], dst.at[k, d - 1], rs_s.at[at], rs_r.at[at], towards(axis, t)))
-        return copies
-
-    def weight_grad(half, k):
-        xh = x // XL if half else XH - 1 - x // XL
-        depth = QN // XH * FEAT
-        r = dot(xt[pl.ds(pl.multiple_of(xh * depth, depth), depth)], g[k]).astype(BF16)
-        for qz in range(N):
-            for xl in range(XL):
-                for yy in range(N):
-                    at = (xh * XL + xl, yy, qz)
-                    o = ((qz * XL + xl) * N + yy) * 16
-                    part[k, at[k % 3], at[(k + 1) % 3], at[(k + 2) % 3]] = r[o:o + 16]
-        xs_here = pl.ds(xh * XL, XL)
+    def item_home():
+        for copy in ig_recv:
+            copy.wait_recv()
+        item_grad = pigf[0]
+        for n in range(len(near_items)):
+            item_grad = item_grad + rig[n].astype(F32)
+        ig_ref[...] = item_grad
+        item_normed = inorm[...]
+        radial = jnp.sum(item_normed * item_grad, axis=1, keepdims=True)
+        gi[0, 0] = ((item_grad - item_normed * radial) / ilen[:, 0:1]).astype(BF16)
+        for n, d in enumerate(near_items):
+            pltpu.make_async_remote_copy(
+                src_ref=gi.at[0, 0], dst_ref=gi.at[0, item_slot(*d)], send_sem=gi_s.at[n], recv_sem=gi_r.at[n],
+                device_id=item_peer(*d), device_id_type=MESH,
+            ).start()
+
+    depth = QN // XH * FEAT
+
+    def weight_grad(m, _):
+        half, k = m // COLOURS, lax.rem(m, COLOURS)
+        xh = jnp.where(half == 0, XH - 1 - x // XL, x // XL)
+
+        @pl.when(half == 0)
+        def _():
+            arrived(g.at[k, pl.ds(ROWS, ROWS)], g_r.at[k])
+
+        pl.when(m == HOME)(item_home)
+        r = dot(xt[pl.ds(pl.multiple_of(xh * depth, depth), depth)], g[k])
+        part[k, xh] = r.astype(BF16).reshape(N, XL, N, 16, CW)
+
+        def go(src, dst, sems, to):
+            pltpu.make_async_remote_copy(
+                src_ref=src, dst_ref=dst, send_sem=ra_s.at[sems], recv_sem=ra_r.at[sems], device_id=to,
+                device_id_type=MESH,
+            ).start()
+
+        for xl in range(XL):
+            t = xh * XL + xl
+            d = lax.rem(t - x + N, N) - 1
+
+            @pl.when((k == 0) & (t != x))
+            def _(t=t, xl=xl, d=d):
+                go(part.at[0, xh, :, xl], ra0.at[d], (0, d, 0), towards(0, t))
+
+        @pl.when(k == 1)
+        def _():
+            for d in steps:
+                t = plus(y, d, N)
+                go(part.at[1, xh, :, :, t], ra1.at[d - 1, xh], (1, d - 1, half), towards(1, t))
+
+        @pl.when(k == 2)
+        def _():
+            for d in steps:
+                t = plus(z, d, N)
+                go(part.at[2, xh, t], ra2.at[d - 1, xh], (2, d - 1, half), towards(2, t))
+
+        return 0
+
+    def slabs(k, d):
         if k == 0:
-            for t in ([pair_a] if half else [xh * XL + xl for xl in range(XL)]):
-                d = lax.rem(t - x + N, N) - 1
-                send(part.at[0, t], ra.at[0, d], ra_s.at[0, d, 0], ra_r.at[0, d, 0], towards(0, t))
-            return
-        for d in range(1, N):
-            t = plus(pos[k], d, N)
-            if k == 1:
-                src, dst = part.at[1, t, :, xs_here], ra.at[1, d - 1, :, xs_here]
-            else:
-                src, dst = part.at[2, t, xs_here], ra.at[2, d - 1, xs_here]
-            send(src, dst, ra_s.at[k, d - 1, half], ra_r.at[k, d - 1, half], towards(k, t))
-
-    def wait_slabs(k):
+            return [ra0.at[d]]
+        return [(ra1 if k == 1 else ra2).at[d, h] for h in range(XH)]
+
+    lax.fori_loop(0, COLOURS, backward, 0)
+    for copy in loss_copies:
+        copy.wait_recv()
+    loss_copies = reduce_loss(reduced_loss(0), 1, y)
+    lax.fori_loop(0, 2 * COLOURS, weight_grad, 0)
+    for copy in loss_copies:
+        copy.wait_recv()
+    loss_copies = reduce_loss(reduced_loss(1), 2, z)
+    flight = {}
+
+    def add_a(k):
         for d in range(N - 1):
-            if k == 0:
-                slabs = [ra.at[0, d]]
-            elif k == 1:
-                slabs = [ra.at[1, d, :, pl.ds(h * XL, XL)] for h in range(XH)]
-            else:
-                slabs = [ra.at[2, d, pl.ds(h * XL, XL)] for h in range(XH)]
-            for h, slab in enumerate(slabs):
-                pltpu.make_async_remote_copy(
-                    src_ref=slab, dst_ref=slab, send_sem=ra_s.at[k, d, h], recv_sem=ra_r.at[k, d, h],
-                    device_id=sibling, device_id_type=MESH,
-                ).wait_recv()
-
-    g_copies = [backward(0), backward(1)]
-    for copy in loss_copies:
-        copy.wait_recv()
-    loss_copies = reduce_loss(reduced_loss(0), 1, y)
-    g_copies[0].wait_recv()
-    weight_grad(0, 0)
-    g_copies.append(backward(2))
-    g_copies[1].wait_recv()
-    weight_grad(0, 1)
-    g_copies[2].wait_recv()
-    weight_grad(0, 2)
-
-    for copy in ig_recv:
-        copy.wait_recv()
-    item_grad = pigf[0]
-    for n in range(len(near_items)):
-        item_grad = item_grad + rig[n].astype(F32)
-    ig_ref[...] = item_grad
-    item_normed = inorm[...]
-    radial = jnp.sum(item_normed * item_grad, axis=1, keepdims=True)
-    gi[0, 0] = ((item_grad - item_normed * radial) / ilen[:, 0:1]).astype(BF16)
-    gi_recv = []
-    for d in range(1, N):
-        to = device(x, y, plus(z, d, N), c)
-        gi_recv.append(send(gi.at[0, 0], gi.at[0, d], gi_s.at[d - 1], gi_r.at[d - 1], to))
-    for k in range(COLOURS):
-        weight_grad(1, k)
-    for copy in loss_copies:
-        copy.wait_recv()
-    loss_copies = reduce_loss(reduced_loss(1), 2, z)
-    for copy in gi_recv:
-        copy.wait_recv()
-    gi_hop = send(gi.at[0], gi.at[1], hop_s.at[2], hop_r.at[2], sibling)
-
-    flight = {}
-
-    def add_a(k):
-        wait_slabs(k)
-        me = pos[k % 3]
+            for h, slab in enumerate(slabs(k, d)):
+                arrived(slab, ra_r.at[k, d, h])
+        p1, p2 = pos[(k + 1) % 3], pos[(k + 2) % 3]
 
         def step(n, _):
             i, j = n // N, lax.rem(n, N)
-            total = part[k, me, i, j].astype(F32)
+            if k == 0:
+                own, got = part.at[0, x // XL, j, lax.rem(x, XL), i], lambda d: ra0[d, j, i]
+            elif k == 1:
+                own, got = part.at[1, j // XL, i, lax.rem(j, XL), y], lambda d: ra1[d, j // XL, i, lax.rem(j, XL)]
+            else:
+                own, got = part.at[2, i // XL, z, lax.rem(i, XL), j], lambda d: ra2[d, i // XL, lax.rem(i, XL), j]
+            total = own[...].astype(F32)
             for d in range(N - 1):
-                total = total + ra[k, d, i, j].astype(F32)
+                total = total + got(d).astype(F32)
             sa[k, i, j] = total.astype(BF16)
             return 0
 
         lax.fori_loop(0, N * N, step, 0)
-        flight[k] = phase(k, 1, sa, rb)
+        flight[k] = []
+        for n, (di, dj) in enumerate(planes):
+            at = list(pos)
+            i, j = plus(p1, di, N), plus(p2, dj, N)
+            at[(k + 1) % 3], at[(k + 2) % 3] = i, j
+            to = device(at[0], at[1], at[2], c)
+            flight[k].append(send(sa.at[k, i, j], rb.at[k, n], rs_s.at[k, n], rs_r.at[k, n], to))
 
     def add_b(k):
         for copy in flight[k]:
             copy.wait_recv()
-        me = pos[(k + 1) % 3]
-        for j in range(N):
-            total = sa[k, me, j].astype(F32)
-            for d in range(N - 1):
-                total = total + rb[k, d, j].astype(F32)
-            sb[k, j] = total.astype(BF16)
-        flight[k] = phase(k, 2, sb, rc)
-
-    def add_c(k):
-        for copy in flight[k]:
-            copy.wait_recv()
-        total = sb[k, pos[(k + 2) % 3]].astype(F32)
-        for d in range(N - 1):
-            total = total + rc[k, d].astype(F32)
+        total = sa[k, pos[(k + 1) % 3], pos[(k + 2) % 3]].astype(F32)
+        for n in range(len(planes)):
+            total = total + rb[k, n].astype(F32)
         gu_ref[:, k * CW:(k + 1) * CW] = total
 
     add_a(0)
+    for n, d in enumerate(near_items):
+        arrived(gi.at[0, item_slot(*d)], gi_r.at[n])
+    gi_hop = send(gi.at[0], gi.at[1], hop_s.at[2], hop_r.at[2], sibling)
     add_a(1)
+    for copy in xi_recv:
+        copy.wait_recv()
+    gi_hop.wait_recv()
+    r = dot_t(xi[...].reshape(NI * USERS, FEAT), gi[...].reshape(NI * USERS, E)).astype(BF16)
+    parti[...] = r.reshape(NU, 16, E)
+    ri_recv = []
+    for n, d in enumerate(user_peers):
+        ri_recv.append(send(parti.at[user_slot(*d)], ri.at[n], ri_s.at[n], ri_r.at[n], user_peer(*d)))
     add_a(2)
     for copy in loss_copies:
         copy.wait_recv()
     corelosses[c] = reduced_loss(2)
     core_copy = send(corelosses.at[c], corelosses.at[c], hop_s.at[3], hop_r.at[3], sibling)
-    for copy in xi_recv:
-        copy.wait_recv()
-    gi_hop.wait_recv()
-    for h in range(XH):
-        r = dot_t(
-            xi[h].reshape(N * CORES * USERS, FEAT), gi[...].reshape(N * CORES * USERS, E)
-        ).astype(BF16)
-        for xl in range(XL):
-            for yy in range(N):
-                o = (xl * N + yy) * 16
-                parti[h * XL + xl, yy] = r[o:o + 16]
-    ri_recv = []
-    for n, (dx, dy) in enumerate(row_peers):
-        tx, ty = plus(x, dx, N), plus(y, dy, N)
-        ri_recv.append(send(parti.at[tx, ty], ri.at[n], ri_s.at[n], ri_r.at[n], row_peer(dx, dy)))
     add_b(0)
     add_b(1)
-    add_b(2)
     core_copy.wait_recv()
     loss_ref[...] = jnp.broadcast_to(jnp.sum(corelosses[0] + corelosses[1], keepdims=True) / TOTAL, (8, 128))
-    add_c(0)
-    add_c(1)
     for copy in ri_recv:
         copy.wait_recv()
-    total = parti[x, y].astype(F32)
-    for n in range(len(row_peers)):
+    total = parti[my_user_slot].astype(F32)
+    for n in range(len(user_peers)):
         total = total + ri[n].astype(F32)
     gi_ref[...] = total
-    add_c(2)
+    add_b(2)
     for copy in sent:
         copy.wait_send()
+    for k in range(COLOURS):
+        left(g.at[k, pl.ds(0, ROWS)], g_s.at[k])
+        for d in range(N - 1):
+            for h, slab in enumerate(slabs(k, d)):
+                left(slab, ra_s.at[k, d, h])
+    for n in range(len(near_items)):
+        left(gi.at[0, 0], gi_s.at[n])
 
 
 def hand_out(loss, ig, gu, gi, loss_out, ig_out, gu_out, gi_out):
@@ -504,7 +513,7 @@
     total = users * lax.axis_size("blk") * lax.axis_size("group")
     NU, NI, NS, QN = XL * N, XL * N * CORES, XL * N, (N // XL) * N
     feat = depth // (QN * CORES)
-    hbm = pl.BlockSpec(memory_space=pl.ANY)
+    hbm = pl.BlockSpec(memory_space=pltpu.HBM)
     smem = pl.BlockSpec(memory_space=pltpu.SMEM)
     vmem = pl.BlockSpec(memory_space=pltpu.VMEM)
     rows = depth // (N * N * N * CORES)
@@ -526,29 +535,29 @@
         V((CORES, NS, users, E), BF16), V((NS, users, E), F32), V((NS, users, E), BF16),
         V((NS - 1, users, E), BF16),
         V((NU, users, E), BF16), V((NU - 1, users, E), BF16),
-        V((COLOURS, 2 * users * hist, CW), BF16), V((CORES, N, users, E), BF16),
-        V((N // XL, N * CORES, users, feat), BF16), V((QN * feat, 2 * users * hist), BF16),
-        V((COLOURS, N, N, N, rows, CW), BF16), V((COLOURS, N - 1, N, N, rows, CW), BF16),
-        V((COLOURS, N, N, rows, CW), BF16), V((COLOURS, N - 1, N, rows, CW), BF16),
-        V((COLOURS, N, rows, CW), BF16), V((COLOURS, N - 1, rows, CW), BF16),
-        V((N, N, rows, E), BF16), V((N * N - 1, rows, E), BF16),
+        V((COLOURS, 2 * users * hist, CW), BF16), V((CORES, NS, users, E), BF16),
+        V((NI, users, feat), BF16), V((QN * feat, 2 * users * hist), BF16),
+        V((COLOURS, N // XL, N, XL, N, rows, CW), BF16), V((N - 1, N, N, rows, CW), BF16),
+        V((N - 1, N // XL, N, XL, rows, CW), BF16), V((N - 1, N // XL, XL, N, rows, CW), BF16),
+        V((COLOURS, N, N, rows, CW), BF16), V((COLOURS, N * N - 1, rows, CW), BF16),
+        V((NU, rows, E), BF16), V((NU - 1, rows, E), BF16),
         V((3, N, 8, 128), F32), V((CORES, 8, 128), F32),
         pltpu.SMEM((1,), F32), pltpu.SMEM((1,), F32), V((1, users), jnp.int32), V((1, users), jnp.int32),
-        dma(8), dma(QN), dma(QN), dma(N * CORES - 1, N // XL), dma(N * CORES - 1, N // XL),
+        dma(8), dma(QN), dma(QN), dma(NI - 1), dma(NI - 1),
         dma(NI - 1), dma(NI - 1), dma(NU - 1), dma(NU - 1), dma(NU - 1), dma(NU - 1),
         dma(NS - 1), dma(NS - 1), dma(NU - 1), dma(NU - 1),
-        dma(NS - 1), dma(NS - 1), dma(NU - 1), dma(NU - 1), dma(COLOURS), dma(COLOURS), dma(N - 1), dma(N - 1),
-        dma(COLOURS, N - 1, 2), dma(COLOURS, N - 1, 2), dma(COLOURS, 2, N - 1), dma(COLOURS, 2, N - 1),
-        dma(N * N - 1), dma(N * N - 1), dma(3, N - 1), dma(3, N - 1), dma(4), dma(4),
+        dma(NS - 1), dma(NS - 1), dma(NU - 1), dma(NU - 1), dma(COLOURS), dma(COLOURS), dma(NS - 1), dma(NS - 1),
+        dma(COLOURS, N - 1, 2), dma(COLOURS, N - 1, 2), dma(COLOURS, N * N - 1), dma(COLOURS, N * N - 1),
+        dma(NU - 1), dma(NU - 1), dma(3, N - 1), dma(3, N - 1), dma(4), dma(4),
     ]
     outs = pl.pallas_call(
         functools.partial(tower_kernel, N, XL, total),
         name="two_tower",
         out_shape=(
-            jax.ShapeDtypeStruct((8, 128), F32),
-            jax.ShapeDtypeStruct((users, E), F32),
-            jax.ShapeDtypeStruct((rows, E), F32),
-            jax.ShapeDtypeStruct((rows, E), F32),
+            pltpu.VMEM((8, 128), F32),
+            pltpu.VMEM((users, E), F32),
+            pltpu.VMEM((rows, E), F32),
+            pltpu.VMEM((rows, E), F32),
         ),
         in_specs=[hbm] * 8,
         out_specs=(vmem,) * 4,
@@ -571,6 +580,7 @@
         ),
         in_specs=[vmem] * 4,
         out_specs=(smem, vmem, vmem, vmem),
+        compiler_params=pltpu.CompilerParams(vmem_limit_bytes=4 * 1024 * 1024),
     )(*outs)
 
 

time: 61.8 us -> 59.5 us (0.963); the launches traced: 61.6 us -> 58.5 us
  Pallas kernels: 59.7 us -> 56.5 us
    pallas_call x1, Pallas kernels: 58.1 us -> 55.8 us  [shards(): pl.pallas_call(functools.partial(tower_kernel, N, XL, total), name='two_t...]
    pallas_call x1, Pallas kernels: 1.58 us -> 0.68 us  [shards(): pl.pallas_call(hand_out, name='hand_out', out_shape=(jax.ShapeDtypeStruct...]
where the time goes in v4:
time: 59.5 us; the launch traced here: 58.5 us
  Pallas kernels  56.5 us (95%)
  between operations  1.93 us (3%)
    pallas_call x1, Pallas kernels, shards(): pl.pallas_call(functools.partial(tower_kernel, N, XL, total), name='two_t...  55.8 us

profile of v4, /device:TPU:0, one launch (start us, length us, event | category | flops | bytes accessed | tf_op | source)
XLA Modules:
  0.0 58.5 jit_solution(2364379055265361387)
XLA Ops:
  1.9 55.8 %two_tower.1 = (f32[8,128]{1,0:T(8,128)S(1)}, f32[32,768]{1,0:T(8,128)S(1)}, f32[16,768]{1,0:T(8,128)S(1)}, f32[16,768]{1,0:T(8,128)S(1)}) custom-call(bf16[768,2048]{1,0:T(8,128)(2,1)} %bitcast.3, bf16[32,2048]{1,0:T(8,128)(2,1)} %ci_hbm.1, bf16[2048,768]{1,0:T(8,128)(2,1)} %wu_hbm.1, bf16[2048,768]{1,0:T(8,128)(2,1)} %wi_hbm.1, f32[1]{0:T(128)S(6)} %copy.12.scale_ref, ...), custom_call_target="tpu_custom_call" | custom-call | tf_op jit(solution)/shard_map/two_tower/pallas_call | solution.py:553
  57.8 0.7 %hand_out.1 = (f32[1]{0:T(128)}, f32[32,768]{1,0:T(8,128)}, f32[16,768]{1,0:T(8,128)}, f32[16,768]{1,0:T(8,128)}) custom-call(f32[8,128]{1,0:T(8,128)S(1)} %get-tuple-element.8.loss, f32[32,768]{1,0:T(8,128)S(1)} %get-tuple-element.9.ig, f32[16,768]{1,0:T(8,128)S(1)} %get-tuple-element.10.gu, f32[16,768]{1,0:T(8,128)S(1)} %get-tuple-element.11.gi), custom_call_target="tpu_custom_call" | custom-call | tf_op jit(solution)/shard_map/hand_out/pallas_call | solution.py:572

commit v5 on v4

--- a/solution.py
+++ b/solution.py
@@ -13,7 +13,6 @@
 BF16 = jnp.bfloat16
 CORES = 2
 COLOURS = 3
-HOME = 2
 
 
 def dot(a, b):
@@ -264,8 +263,8 @@
     for copy in ua_recv:
         copy.wait_recv()
     ia_hop.wait_recv()
-    scale = scale_s[0]
-    shift = shift_s[0]
+    scale = scale_s[0, 0]
+    shift = shift_s[0, 0]
     users = ua[...].reshape(NU * USERS, E)
     loss = jnp.zeros((8, 128), F32)
     for n in range(NI // N):
@@ -327,7 +326,8 @@
 
     pos = (x, y, z)
 
-    def backward(k, _):
+    def backward(m, _):
+        k = jnp.where(m < 2, 1 - m, m)
         cols = pl.ds(pl.multiple_of(k * CW, CW), CW)
 
         def step(u, _):
@@ -366,58 +366,38 @@
                 device_id=item_peer(*d), device_id_type=MESH,
             ).start()
 
-    depth = QN // XH * FEAT
-
     def weight_grad(m, _):
-        half, k = m // COLOURS, lax.rem(m, COLOURS)
-        xh = jnp.where(half == 0, XH - 1 - x // XL, x // XL)
-
-        @pl.when(half == 0)
-        def _():
-            arrived(g.at[k, pl.ds(ROWS, ROWS)], g_r.at[k])
-
-        pl.when(m == HOME)(item_home)
-        r = dot(xt[pl.ds(pl.multiple_of(xh * depth, depth), depth)], g[k])
-        part[k, xh] = r.astype(BF16).reshape(N, XL, N, 16, CW)
-
-        def go(src, dst, sems, to):
-            pltpu.make_async_remote_copy(
-                src_ref=src, dst_ref=dst, send_sem=ra_s.at[sems], recv_sem=ra_r.at[sems], device_id=to,
-                device_id_type=MESH,
-            ).start()
-
-        for xl in range(XL):
-            t = xh * XL + xl
-            d = lax.rem(t - x + N, N) - 1
-
-            @pl.when((k == 0) & (t != x))
-            def _(t=t, xl=xl, d=d):
-                go(part.at[0, xh, :, xl], ra0.at[d], (0, d, 0), towards(0, t))
-
-        @pl.when(k == 1)
-        def _():
-            for d in steps:
-                t = plus(y, d, N)
-                go(part.at[1, xh, :, :, t], ra1.at[d - 1, xh], (1, d - 1, half), towards(1, t))
-
-        @pl.when(k == 2)
-        def _():
-            for d in steps:
-                t = plus(z, d, N)
-                go(part.at[2, xh, t], ra2.at[d - 1, xh], (2, d - 1, half), towards(2, t))
+        k = jnp.where(m < 2, 1 - m, m)
+        pl.when(m == 1)(item_home)
+        arrived(g.at[k, pl.ds(ROWS, ROWS)], g_r.at[k])
+        part[k] = dot(xt[...], g[k]).astype(BF16).reshape(XH, N, XL, N, 16, CW)
+        for axis in range(COLOURS):
+
+            @pl.when(k == axis)
+            def _(axis=axis):
+                for d in steps:
+                    t = plus(pos[axis], d, N)
+                    pltpu.make_async_remote_copy(
+                        src_ref=slab(axis, t), dst_ref=ra[axis].at[d - 1], send_sem=ra_s.at[axis, d - 1],
+                        recv_sem=ra_r.at[axis, d - 1], device_id=towards(axis, t), device_id_type=MESH,
+                    ).start()
 
         return 0
 
-    def slabs(k, d):
-        if k == 0:
-            return [ra0.at[d]]
-        return [(ra1 if k == 1 else ra2).at[d, h] for h in range(XH)]
+    ra = (ra0, ra1, ra2)
+
+    def slab(axis, t):
+        if axis == 0:
+            return part.at[0, t // XL, :, lax.rem(t, XL)]
+        if axis == 1:
+            return part.at[1, :, :, :, t]
+        return part.at[2, :, t]
 
     lax.fori_loop(0, COLOURS, backward, 0)
     for copy in loss_copies:
         copy.wait_recv()
     loss_copies = reduce_loss(reduced_loss(0), 1, y)
-    lax.fori_loop(0, 2 * COLOURS, weight_grad, 0)
+    lax.fori_loop(0, COLOURS, weight_grad, 0)
     for copy in loss_copies:
         copy.wait_recv()
     loss_copies = reduce_loss(reduced_loss(1), 2, z)
@@ -425,8 +405,7 @@
 
     def add_a(k):
         for d in range(N - 1):
-            for h, slab in enumerate(slabs(k, d)):
-                arrived(slab, ra_r.at[k, d, h])
+            arrived(ra[k].at[d], ra_r.at[k, d])
         p1, p2 = pos[(k + 1) % 3], pos[(k + 2) % 3]
 
         def step(n, _):
@@ -460,7 +439,6 @@
             total = total + rb[k, n].astype(F32)
         gu_ref[:, k * CW:(k + 1) * CW] = total
 
-    add_a(0)
     for n, d in enumerate(near_items):
         arrived(gi.at[0, item_slot(*d)], gi_r.at[n])
     gi_hop = send(gi.at[0], gi.at[1], hop_s.at[2], hop_r.at[2], sibling)
@@ -473,13 +451,14 @@
     ri_recv = []
     for n, d in enumerate(user_peers):
         ri_recv.append(send(parti.at[user_slot(*d)], ri.at[n], ri_s.at[n], ri_r.at[n], user_peer(*d)))
+    add_a(0)
     add_a(2)
     for copy in loss_copies:
         copy.wait_recv()
     corelosses[c] = reduced_loss(2)
     core_copy = send(corelosses.at[c], corelosses.at[c], hop_s.at[3], hop_r.at[3], sibling)
+    add_b(1)
     add_b(0)
-    add_b(1)
     core_copy.wait_recv()
     loss_ref[...] = jnp.broadcast_to(jnp.sum(corelosses[0] + corelosses[1], keepdims=True) / TOTAL, (8, 128))
     for copy in ri_recv:
@@ -494,8 +473,7 @@
     for k in range(COLOURS):
         left(g.at[k, pl.ds(0, ROWS)], g_s.at[k])
         for d in range(N - 1):
-            for h, slab in enumerate(slabs(k, d)):
-                left(slab, ra_s.at[k, d, h])
+            left(ra[k].at[d], ra_s.at[k, d])
     for n in range(len(near_items)):
         left(gi.at[0, 0], gi_s.at[n])
 
@@ -542,12 +520,12 @@
         V((COLOURS, N, N, rows, CW), BF16), V((COLOURS, N * N - 1, rows, CW), BF16),
         V((NU, rows, E), BF16), V((NU - 1, rows, E), BF16),
         V((3, N, 8, 128), F32), V((CORES, 8, 128), F32),
-        pltpu.SMEM((1,), F32), pltpu.SMEM((1,), F32), V((1, users), jnp.int32), V((1, users), jnp.int32),
+        V((1, 1), F32), V((1, 1), F32), V((1, users), jnp.int32), V((1, users), jnp.int32),
         dma(8), dma(QN), dma(QN), dma(NI - 1), dma(NI - 1),
         dma(NI - 1), dma(NI - 1), dma(NU - 1), dma(NU - 1), dma(NU - 1), dma(NU - 1),
         dma(NS - 1), dma(NS - 1), dma(NU - 1), dma(NU - 1),
         dma(NS - 1), dma(NS - 1), dma(NU - 1), dma(NU - 1), dma(COLOURS), dma(COLOURS), dma(NS - 1), dma(NS - 1),
-        dma(COLOURS, N - 1, 2), dma(COLOURS, N - 1, 2), dma(COLOURS, N * N - 1), dma(COLOURS, N * N - 1),
+        dma(COLOURS, N - 1), dma(COLOURS, N - 1), dma(COLOURS, N * N - 1), dma(COLOURS, N * N - 1),
         dma(NU - 1), dma(NU - 1), dma(3, N - 1), dma(3, N - 1), dma(4), dma(4),
     ]
     outs = pl.pallas_call(
@@ -566,7 +544,7 @@
             collective_id=0, has_side_effects=True, vmem_limit_bytes=60 * 1024 * 1024
         ),
     )(
-        past.reshape(users * hist, depth), cand, wu, wi, scale, shift,
+        past.reshape(users * hist, depth), cand, wu, wi, scale.reshape(1, 1), shift.reshape(1, 1),
         ids.reshape(1, users), slots.reshape(1, users),
     )
     return pl.pallas_call(

time: 59.5 us -> 57.5 us (0.966)
  Pallas kernels: 56.5 us -> 54.7 us
    pallas_call x1, Pallas kernels: 55.8 us -> 54 us  [shards(): pl.pallas_call(functools.partial(tower_kernel, N, XL, total), name='two_t...]
where the time goes in v5:
time: 57.5 us; the launch traced here: 56.6 us
  Pallas kernels  54.7 us (95%)
  between operations  1.93 us (3%)
    pallas_call x1, Pallas kernels, shards(): pl.pallas_call(functools.partial(tower_kernel, N, XL, total), name='two_t...  54 us

profile of v5, /device:TPU:0, one launch (start us, length us, event | category | flops | bytes accessed | tf_op | source)
XLA Modules:
  0.0 56.6 jit_solution(16722123664767626020)
XLA Ops:
  1.9 54.0 %two_tower.1 = (f32[8,128]{1,0:T(8,128)S(1)}, f32[32,768]{1,0:T(8,128)S(1)}, f32[16,768]{1,0:T(8,128)S(1)}, f32[16,768]{1,0:T(8,128)S(1)}) custom-call(bf16[768,2048]{1,0:T(8,128)(2,1)} %bitcast.7, bf16[32,2048]{1,0:T(8,128)(2,1)} %ci_hbm.1, bf16[2048,768]{1,0:T(8,128)(2,1)} %wu_hbm.1, bf16[2048,768]{1,0:T(8,128)(2,1)} %wi_hbm.1, f32[1,1]{1,0:T(1,128)} %bitcast.5.scale_ref, ...), custom_call_target="tpu_custom_call" | custom-call | tf_op jit(solution)/shard_map/two_tower/pallas_call | solution.py:531
  55.9 0.7 %hand_out.1 = (f32[1]{0:T(128)}, f32[32,768]{1,0:T(8,128)}, f32[16,768]{1,0:T(8,128)}, f32[16,768]{1,0:T(8,128)}) custom-call(f32[8,128]{1,0:T(8,128)S(1)} %get-tuple-element.8.loss, f32[32,768]{1,0:T(8,128)S(1)} %get-tuple-element.9.ig, f32[16,768]{1,0:T(8,128)S(1)} %get-tuple-element.10.gu, f32[16,768]{1,0:T(8,128)S(1)} %get-tuple-element.11.gi), custom_call_target="tpu_custom_call" | custom-call | tf_op jit(solution)/shard_map/hand_out/pallas_call | solution.py:550

commit v6 on v5

--- a/solution.py
+++ b/solution.py
@@ -28,7 +28,7 @@
 
 
 def sigmoid(v):
-    return 1.0 / (1.0 + jnp.exp(-v))
+    return 0.5 + 0.5 * jnp.tanh(0.5 * v)
 
 
 def tower_kernel(
@@ -407,9 +407,9 @@
         for d in range(N - 1):
             arrived(ra[k].at[d], ra_r.at[k, d])
         p1, p2 = pos[(k + 1) % 3], pos[(k + 2) % 3]
-
-        def step(n, _):
-            i, j = n // N, lax.rem(n, N)
+        flight[k] = []
+        for n, (di, dj) in enumerate(planes + [(0, 0)]):
+            i, j = plus(p1, di, N), plus(p2, dj, N)
             if k == 0:
                 own, got = part.at[0, x // XL, j, lax.rem(x, XL), i], lambda d: ra0[d, j, i]
             elif k == 1:
@@ -419,30 +419,25 @@
             total = own[...].astype(F32)
             for d in range(N - 1):
                 total = total + got(d).astype(F32)
-            sa[k, i, j] = total.astype(BF16)
-            return 0
-
-        lax.fori_loop(0, N * N, step, 0)
-        flight[k] = []
-        for n, (di, dj) in enumerate(planes):
-            at = list(pos)
-            i, j = plus(p1, di, N), plus(p2, dj, N)
-            at[(k + 1) % 3], at[(k + 2) % 3] = i, j
-            to = device(at[0], at[1], at[2], c)
-            flight[k].append(send(sa.at[k, i, j], rb.at[k, n], rs_s.at[k, n], rs_r.at[k, n], to))
+            sa[k, n] = total.astype(BF16)
+            if (di, dj) != (0, 0):
+                at = list(pos)
+                at[(k + 1) % 3], at[(k + 2) % 3] = i, j
+                to = device(at[0], at[1], at[2], c)
+                flight[k].append(send(sa.at[k, n], rb.at[k, n], rs_s.at[k, n], rs_r.at[k, n], to))
 
     def add_b(k):
         for copy in flight[k]:
             copy.wait_recv()
-        total = sa[k, pos[(k + 1) % 3], pos[(k + 2) % 3]].astype(F32)
+        total = sa[k, len(planes)].astype(F32)
         for n in range(len(planes)):
             total = total + rb[k, n].astype(F32)
         gu_ref[:, k * CW:(k + 1) * CW] = total
 
+    add_a(1)
     for n, d in enumerate(near_items):
         arrived(gi.at[0, item_slot(*d)], gi_r.at[n])
     gi_hop = send(gi.at[0], gi.at[1], hop_s.at[2], hop_r.at[2], sibling)
-    add_a(1)
     for copy in xi_recv:
         copy.wait_recv()
     gi_hop.wait_recv()
@@ -457,17 +452,6 @@
         copy.wait_recv()
     corelosses[c] = reduced_loss(2)
     core_copy = send(corelosses.at[c], corelosses.at[c], hop_s.at[3], hop_r.at[3], sibling)
-    add_b(1)
-    add_b(0)
-    core_copy.wait_recv()
-    loss_ref[...] = jnp.broadcast_to(jnp.sum(corelosses[0] + corelosses[1], keepdims=True) / TOTAL, (8, 128))
-    for copy in ri_recv:
-        copy.wait_recv()
-    total = parti[my_user_slot].astype(F32)
-    for n in range(len(user_peers)):
-        total = total + ri[n].astype(F32)
-    gi_ref[...] = total
-    add_b(2)
     for copy in sent:
         copy.wait_send()
     for k in range(COLOURS):
@@ -476,6 +460,17 @@
             left(ra[k].at[d], ra_s.at[k, d])
     for n in range(len(near_items)):
         left(gi.at[0, 0], gi_s.at[n])
+    add_b(1)
+    add_b(0)
+    core_copy.wait_recv()
+    loss_ref[...] = jnp.broadcast_to(jnp.sum(corelosses[0] + corelosses[1], keepdims=True) / TOTAL, (8, 128))
+    for copy in ri_recv:
+        copy.wait_recv()
+    total = parti[my_user_slot].astype(F32)
+    for n in range(len(user_peers)):
+        total = total + ri[n].astype(F32)
+    gi_ref[...] = total
+    add_b(2)
 
 
 def hand_out(loss, ig, gu, gi, loss_out, ig_out, gu_out, gi_out):
@@ -517,7 +512,7 @@
         V((NI, users, feat), BF16), V((QN * feat, 2 * users * hist), BF16),
         V((COLOURS, N // XL, N, XL, N, rows, CW), BF16), V((N - 1, N, N, rows, CW), BF16),
         V((N - 1, N // XL, N, XL, rows, CW), BF16), V((N - 1, N // XL, XL, N, rows, CW), BF16),
-        V((COLOURS, N, N, rows, CW), BF16), V((COLOURS, N * N - 1, rows, CW), BF16),
+        V((COLOURS, N * N, rows, CW), BF16), V((COLOURS, N * N - 1, rows, CW), BF16),
         V((NU, rows, E), BF16), V((NU - 1, rows, E), BF16),
         V((3, N, 8, 128), F32), V((CORES, 8, 128), F32),
         V((1, 1), F32), V((1, 1), F32), V((1, users), jnp.int32), V((1, users), jnp.int32),

time: 57.5 us -> 56.5 us (0.983); the launches traced: 56.6 us -> 56.3 us
  no operation moved by 1% of the time
where the time goes in v6:
time: 56.5 us; the launch traced here: 56.3 us
  Pallas kernels  54.4 us (96%)
  between operations  1.93 us (3%)
    pallas_call x1, Pallas kernels, shards(): pl.pallas_call(functools.partial(tower_kernel, N, XL, total), name='two_t...  53.7 us

profile of v6, /device:TPU:0, one launch (start us, length us, event | category | flops | bytes accessed | tf_op | source)
XLA Modules:
  0.0 56.3 jit_solution(11838714563389400846)
XLA Ops:
  1.9 53.7 %two_tower.1 = (f32[8,128]{1,0:T(8,128)S(1)}, f32[32,768]{1,0:T(8,128)S(1)}, f32[16,768]{1,0:T(8,128)S(1)}, f32[16,768]{1,0:T(8,128)S(1)}) custom-call(bf16[768,2048]{1,0:T(8,128)(2,1)} %bitcast.7, bf16[32,2048]{1,0:T(8,128)(2,1)} %ci_hbm.1, bf16[2048,768]{1,0:T(8,128)(2,1)} %wu_hbm.1, bf16[2048,768]{1,0:T(8,128)(2,1)} %wi_hbm.1, f32[1,1]{1,0:T(1,128)} %bitcast.5.scale_ref, ...), custom_call_target="tpu_custom_call" | custom-call | tf_op jit(solution)/shard_map/two_tower/pallas_call | solution.py:526
  55.6 0.7 %hand_out.1 = (f32[1]{0:T(128)}, f32[32,768]{1,0:T(8,128)}, f32[16,768]{1,0:T(8,128)}, f32[16,768]{1,0:T(8,128)}) custom-call(f32[8,128]{1,0:T(8,128)S(1)} %get-tuple-element.8.loss, f32[32,768]{1,0:T(8,128)S(1)} %get-tuple-element.9.ig, f32[16,768]{1,0:T(8,128)S(1)} %get-tuple-element.10.gu, f32[16,768]{1,0:T(8,128)S(1)} %get-tuple-element.11.gi), custom_call_target="tpu_custom_call" | custom-call | tf_op jit(solution)/shard_map/hand_out/pallas_call | solution.py:545

commit v7 on v6

--- a/solution.py
+++ b/solution.py
@@ -39,7 +39,7 @@
     ua, ia, idrow, idbuf, slotbuf, tgtbuf, wt, pig, pigf, rigc, rig, pgu, rgu, g, gi, xi, xt,
     part, ra0, ra1, ra2, sa, rb, parti, ri, losses, corelosses, scale_s, shift_s, idv, slotv,
     lsem, xsem_s, xsem_r, xi_s, xi_r, id_s, id_r, slot_s, slot_r, tgt_s, tgt_r,
-    ia_s, ia_r, ua_s, ua_r, ig_s, ig_r, ug_s, ug_r, g_s, g_r, gi_s, gi_r,
+    ia_s, ia_r, ua_s, ua_r, ig_s, ig_r, ug_s, ug_r, g_s, g_r, gi_s, gi_r, gh_s, gh_r,
     ra_s, ra_r, rs_s, rs_r, ri_s, ri_r, lo_s, lo_r, hop_s, hop_r,
 ):
     USERS, E = pooled.shape
@@ -102,6 +102,7 @@
     item_peers = near_items + [(db, dz, 1) for db in range(2) for dz in span]
     planes = [(di, dj) for di in span for dj in span if (di, dj) != (0, 0)]
     planes.sort(key=lambda p: -ring(p[0]) - ring(p[1]))
+    feat_peers = [(dz, dc) for dc in range(CORES) for dz in span if (dz, dc) != (0, 0)]
     steps = sorted(range(1, N), key=lambda d: -ring(d))
 
     def user_peer(da, dy):
@@ -233,13 +234,15 @@
         ua_recv.append(send(ua.at[my_user_slot], ua.at[my_user_slot], ua_s.at[n], ua_r.at[n], user_peer(*d)))
 
     xi_recv = []
-    for n, (db, dz, dc) in enumerate(item_peers):
-        px, pz, pc = pair_b if db else x, plus(z, dz, N), plus(c, dc, CORES)
-        cols = pl.ds(pl.multiple_of(((px // XL * N + pz) * CORES + pc) * FEAT, FEAT), FEAT)
-        xi_recv.append(
-            send(civ.at[:, cols], xi.at[item_slot(db, dz, dc)], xi_s.at[n], xi_r.at[n], item_peer(db, dz, dc))
-        )
-    xi[0] = civ[:, pl.ds(pl.multiple_of(((x // XL * N + z) * CORES + c) * FEAT, FEAT), FEAT)]
+    for n, (dz, dc) in enumerate(feat_peers):
+        pz, pc = plus(z, dz, N), plus(c, dc, CORES)
+        for h in range(XH):
+            cols = pl.ds(pl.multiple_of(((h * N + pz) * CORES + pc) * FEAT, FEAT), FEAT)
+            xi_recv.append(
+                send(civ.at[:, cols], xi.at[h, dc * N + dz], xi_s.at[n, h], xi_r.at[n, h], item_peer(0, dz, dc))
+            )
+    for h in range(XH):
+        xi[h, 0] = civ[:, pl.ds(pl.multiple_of(((h * N + z) * CORES + c) * FEAT, FEAT), FEAT)]
     for copy in ia_recv:
         copy.wait_recv()
     ia_hop = send(ia.at[0], ia.at[1], hop_s.at[0], hop_r.at[0], sibling)
@@ -336,13 +339,14 @@
             s = sigmoid(v)
             outer = jnp.broadcast_to(gp[pl.ds(pl.multiple_of(u * 8, 8), 8), cols][:, None, :], (8, HIST, CW))
             g[k, at] = (outer.reshape(8 * HIST, CW) * s * (1.0 + v * (1.0 - s))).astype(BF16)
+            to = pl.ds(pl.multiple_of(ROWS + u * 8 * HIST, 8 * HIST), 8 * HIST)
+            pltpu.make_async_remote_copy(
+                src_ref=g.at[k, at], dst_ref=g.at[k, to], send_sem=g_s.at[k, u], recv_sem=g_r.at[k, u],
+                device_id=sibling, device_id_type=MESH,
+            ).start()
             return 0
 
         lax.fori_loop(0, USERS // 8, step, 0)
-        pltpu.make_async_remote_copy(
-            src_ref=g.at[k, pl.ds(0, ROWS)], dst_ref=g.at[k, pl.ds(ROWS, ROWS)], send_sem=g_s.at[k],
-            recv_sem=g_r.at[k], device_id=sibling, device_id_type=MESH,
-        ).start()
         return 0
 
     def towards(axis, v):
@@ -360,16 +364,24 @@
         item_normed = inorm[...]
         radial = jnp.sum(item_normed * item_grad, axis=1, keepdims=True)
         gi[0, 0] = ((item_grad - item_normed * radial) / ilen[:, 0:1]).astype(BF16)
-        for n, d in enumerate(near_items):
+        gi_hand(0)
+        for d in steps:
             pltpu.make_async_remote_copy(
-                src_ref=gi.at[0, 0], dst_ref=gi.at[0, item_slot(*d)], send_sem=gi_s.at[n], recv_sem=gi_r.at[n],
-                device_id=item_peer(*d), device_id_type=MESH,
+                src_ref=gi.at[0, 0], dst_ref=gi.at[0, d], send_sem=gi_s.at[d], recv_sem=gi_r.at[d],
+                device_id=item_peer(0, d, 0), device_id_type=MESH,
             ).start()
+
+    def gi_hand(d):
+        pltpu.make_async_remote_copy(
+            src_ref=gi.at[0, d], dst_ref=gi.at[1, d], send_sem=gh_s.at[d], recv_sem=gh_r.at[d],
+            device_id=sibling, device_id_type=MESH,
+        ).start()
 
     def weight_grad(m, _):
         k = jnp.where(m < 2, 1 - m, m)
         pl.when(m == 1)(item_home)
-        arrived(g.at[k, pl.ds(ROWS, ROWS)], g_r.at[k])
+        for u in range(USERS // 8):
+            arrived(g.at[k, pl.ds(ROWS + u * 8 * HIST, 8 * HIST)], g_r.at[k, u])
         part[k] = dot(xt[...], g[k]).astype(BF16).reshape(XH, N, XL, N, 16, CW)
         for axis in range(COLOURS):
 
@@ -434,18 +446,21 @@
             total = total + rb[k, n].astype(F32)
         gu_ref[:, k * CW:(k + 1) * CW] = total
 
+    for d in reversed(steps):
+        arrived(gi.at[0, d], gi_r.at[d])
+        gi_hand(d)
+    for copy in xi_recv:
+        copy.wait_recv()
+    for d in range(N):
+        arrived(gi.at[1, d], gh_r.at[d])
+    for h in range(XH):
+        r = dot_t(xi[h].reshape(N * CORES * USERS, FEAT), gi[...].reshape(N * CORES * USERS, E)).astype(BF16)
+        parti[h * XL:(h + 1) * XL] = r.reshape(XL, N, 16, E)
+    ri_recv = []
+    for n, (dx, dy) in enumerate(planes):
+        tx, ty = plus(x, dx, N), plus(y, dy, N)
+        ri_recv.append(send(parti.at[tx, ty], ri.at[n], ri_s.at[n], ri_r.at[n], row_peer(dx, dy)))
     add_a(1)
-    for n, d in enumerate(near_items):
-        arrived(gi.at[0, item_slot(*d)], gi_r.at[n])
-    gi_hop = send(gi.at[0], gi.at[1], hop_s.at[2], hop_r.at[2], sibling)
-    for copy in xi_recv:
-        copy.wait_recv()
-    gi_hop.wait_recv()
-    r = dot_t(xi[...].reshape(NI * USERS, FEAT), gi[...].reshape(NI * USERS, E)).astype(BF16)
-    parti[...] = r.reshape(NU, 16, E)
-    ri_recv = []
-    for n, d in enumerate(user_peers):
-        ri_recv.append(send(parti.at[user_slot(*d)], ri.at[n], ri_s.at[n], ri_r.at[n], user_peer(*d)))
     add_a(0)
     add_a(2)
     for copy in loss_copies:
@@ -455,19 +470,22 @@
     for copy in sent:
         copy.wait_send()
     for k in range(COLOURS):
-        left(g.at[k, pl.ds(0, ROWS)], g_s.at[k])
+        for u in range(USERS // 8):
+            left(g.at[k, pl.ds(u * 8 * HIST, 8 * HIST)], g_s.at[k, u])
         for d in range(N - 1):
             left(ra[k].at[d], ra_s.at[k, d])
-    for n in range(len(near_items)):
-        left(gi.at[0, 0], gi_s.at[n])
+    for d in range(N):
+        left(gi.at[0, d], gh_s.at[d])
+        if d:
+            left(gi.at[0, 0], gi_s.at[d])
     add_b(1)
     add_b(0)
     core_copy.wait_recv()
     loss_ref[...] = jnp.broadcast_to(jnp.sum(corelosses[0] + corelosses[1], keepdims=True) / TOTAL, (8, 128))
     for copy in ri_recv:
         copy.wait_recv()
-    total = parti[my_user_slot].astype(F32)
-    for n in range(len(user_peers)):
+    total = parti[x, y].astype(F32)
+    for n in range(len(planes)):
         total = total + ri[n].astype(F32)
     gi_ref[...] = total
     add_b(2)
@@ -508,20 +526,20 @@
         V((CORES, NS, users, E), BF16), V((NS, users, E), F32), V((NS, users, E), BF16),
         V((NS - 1, users, E), BF16),
         V((NU, users, E), BF16), V((NU - 1, users, E), BF16),
-        V((COLOURS, 2 * users * hist, CW), BF16), V((CORES, NS, users, E), BF16),
-        V((NI, users, feat), BF16), V((QN * feat, 2 * users * hist), BF16),
+        V((COLOURS, 2 * users * hist, CW), BF16), V((CORES, N, users, E), BF16),
+        V((N // XL, N * CORES, users, feat), BF16), V((QN * feat, 2 * users * hist), BF16),
         V((COLOURS, N // XL, N, XL, N, rows, CW), BF16), V((N - 1, N, N, rows, CW), BF16),
         V((N - 1, N // XL, N, XL, rows, CW), BF16), V((N - 1, N // XL, XL, N, rows, CW), BF16),
         V((COLOURS, N * N, rows, CW), BF16), V((COLOURS, N * N - 1, rows, CW), BF16),
-        V((NU, rows, E), BF16), V((NU - 1, rows, E), BF16),
+        V((N, N, rows, E), BF16), V((N * N - 1, rows, E), BF16),
         V((3, N, 8, 128), F32), V((CORES, 8, 128), F32),
         V((1, 1), F32), V((1, 1), F32), V((1, users), jnp.int32), V((1, users), jnp.int32),
-        dma(8), dma(QN), dma(QN), dma(NI - 1), dma(NI - 1),
+        dma(8), dma(QN), dma(QN), dma(N * CORES - 1, N // XL), dma(N * CORES - 1, N // XL),
         dma(NI - 1), dma(NI - 1), dma(NU - 1), dma(NU - 1), dma(NU - 1), dma(NU - 1),
         dma(NS - 1), dma(NS - 1), dma(NU - 1), dma(NU - 1),
-        dma(NS - 1), dma(NS - 1), dma(NU - 1), dma(NU - 1), dma(COLOURS), dma(COLOURS), dma(NS - 1), dma(NS - 1),
+        dma(NS - 1), dma(NS - 1), dma(NU - 1), dma(NU - 1), dma(COLOURS, users // 8), dma(COLOURS, users // 8), dma(N), dma(N), dma(N), dma(N),
         dma(COLOURS, N - 1), dma(COLOURS, N - 1), dma(COLOURS, N * N - 1), dma(COLOURS, N * N - 1),
-        dma(NU - 1), dma(NU - 1), dma(3, N - 1), dma(3, N - 1), dma(4), dma(4),
+        dma(N * N - 1), dma(N * N - 1), dma(3, N - 1), dma(3, N - 1), dma(4), dma(4),
     ]
     outs = pl.pallas_call(
         functools.partial(tower_kernel, N, XL, total),

time: 56.5 us -> 55.4 us (0.981)
  Pallas kernels: 54.4 us -> 53.3 us
    pallas_call x1, Pallas kernels: 53.7 us -> 52.7 us  [shards(): pl.pallas_call(functools.partial(tower_kernel, N, XL, total), name='two_t...]
where the time goes in v7:
time: 55.4 us; the launch traced here: 55.3 us
  Pallas kernels  53.3 us (96%)
  between operations  1.93 us (3%)
    pallas_call x1, Pallas kernels, shards(): pl.pallas_call(functools.partial(tower_kernel, N, XL, total), name='two_t...  52.7 us

profile of v7, /device:TPU:0, one launch (start us, length us, event | category | flops | bytes accessed | tf_op | source)
XLA Modules:
  0.0 55.3 jit_solution(8861089730437604016)
XLA Ops:
  1.9 52.7 %two_tower.1 = (f32[8,128]{1,0:T(8,128)S(1)}, f32[32,768]{1,0:T(8,128)S(1)}, f32[16,768]{1,0:T(8,128)S(1)}, f32[16,768]{1,0:T(8,128)S(1)}) custom-call(bf16[768,2048]{1,0:T(8,128)(2,1)} %bitcast.7, bf16[32,2048]{1,0:T(8,128)(2,1)} %ci_hbm.1, bf16[2048,768]{1,0:T(8,128)(2,1)} %wu_hbm.1, bf16[2048,768]{1,0:T(8,128)(2,1)} %wi_hbm.1, f32[1,1]{1,0:T(1,128)} %bitcast.5.scale_ref, ...), custom_call_target="tpu_custom_call" | custom-call | tf_op jit(solution)/shard_map/two_tower/pallas_call | solution.py:544
  54.6 0.7 %hand_out.1 = (f32[1]{0:T(128)}, f32[32,768]{1,0:T(8,128)}, f32[16,768]{1,0:T(8,128)}, f32[16,768]{1,0:T(8,128)}) custom-call(f32[8,128]{1,0:T(8,128)S(1)} %get-tuple-element.8.loss, f32[32,768]{1,0:T(8,128)S(1)} %get-tuple-element.9.ig, f32[16,768]{1,0:T(8,128)S(1)} %get-tuple-element.10.gu, f32[16,768]{1,0:T(8,128)S(1)} %get-tuple-element.11.gi), custom_call_target="tpu_custom_call" | custom-call | tf_op jit(solution)/shard_map/hand_out/pallas_call | solution.py:563

commit v8 on v7

--- a/solution.py
+++ b/solution.py
@@ -37,10 +37,10 @@
     loss_ref, ig_ref, gu_ref, gi_ref,
     xv, xs, civ, wuv, wiv, pre, pooled, gp, ulen, inorm, ilen,
     ua, ia, idrow, idbuf, slotbuf, tgtbuf, wt, pig, pigf, rigc, rig, pgu, rgu, g, gi, xi, xt,
-    part, ra0, ra1, ra2, sa, rb, parti, ri, losses, corelosses, scale_s, shift_s, idv, slotv,
+    part, ra0, ra1, ra2, sa, rb, parti, ri, si, rj, losses, corelosses, scale_s, shift_s, idv, slotv,
     lsem, xsem_s, xsem_r, xi_s, xi_r, id_s, id_r, slot_s, slot_r, tgt_s, tgt_r,
     ia_s, ia_r, ua_s, ua_r, ig_s, ig_r, ug_s, ug_r, g_s, g_r, gi_s, gi_r, gh_s, gh_r,
-    ra_s, ra_r, rs_s, rs_r, ri_s, ri_r, lo_s, lo_r, hop_s, hop_r,
+    ra_s, ra_r, rs_s, rs_r, ri_s, ri_r, rj_s, rj_r, lo_s, lo_r, hop_s, hop_r,
 ):
     USERS, E = pooled.shape
     HIST = xv.shape[0] // USERS
@@ -456,13 +456,34 @@
     for h in range(XH):
         r = dot_t(xi[h].reshape(N * CORES * USERS, FEAT), gi[...].reshape(N * CORES * USERS, E)).astype(BF16)
         parti[h * XL:(h + 1) * XL] = r.reshape(XL, N, 16, E)
+    left_half, right_half = pl.ds(0, E // 2), pl.ds(E // 2, E // 2)
     ri_recv = []
-    for n, (dx, dy) in enumerate(planes):
-        tx, ty = plus(x, dx, N), plus(y, dy, N)
-        ri_recv.append(send(parti.at[tx, ty], ri.at[n], ri_s.at[n], ri_r.at[n], row_peer(dx, dy)))
+    for d in steps:
+        t = plus(x, d, N)
+        src = parti.at[t, :, :, left_half]
+        ri_recv.append(send(src, ri.at[0, d - 1], ri_s.at[0, d - 1], ri_r.at[0, d - 1], towards(0, t)))
+        t = plus(y, d, N)
+        src = parti.at[:, t, :, right_half]
+        ri_recv.append(send(src, ri.at[1, d - 1], ri_s.at[1, d - 1], ri_r.at[1, d - 1], towards(1, t)))
     add_a(1)
     add_a(0)
     add_a(2)
+    for copy in ri_recv:
+        copy.wait_recv()
+    for n in range(N):
+        total = parti[x, n, :, 0:E // 2].astype(F32)
+        for d in range(N - 1):
+            total = total + ri[0, d, n].astype(F32)
+        si[0, n] = total.astype(BF16)
+        total = parti[n, y, :, E // 2:E].astype(F32)
+        for d in range(N - 1):
+            total = total + ri[1, d, n].astype(F32)
+        si[1, n] = total.astype(BF16)
+    ri_recv = []
+    for h in range(2):
+        for d in steps:
+            t = plus(pos[1 - h], d, N)
+            ri_recv.append(send(si.at[h, t], rj.at[h, d - 1], rj_s.at[h, d - 1], rj_r.at[h, d - 1], towards(1 - h, t)))
     for copy in loss_copies:
         copy.wait_recv()
     corelosses[c] = reduced_loss(2)
@@ -484,10 +505,11 @@
     loss_ref[...] = jnp.broadcast_to(jnp.sum(corelosses[0] + corelosses[1], keepdims=True) / TOTAL, (8, 128))
     for copy in ri_recv:
         copy.wait_recv()
-    total = parti[x, y].astype(F32)
-    for n in range(len(planes)):
-        total = total + ri[n].astype(F32)
-    gi_ref[...] = total
+    for h in range(2):
+        total = si[h, pos[1 - h]].astype(F32)
+        for d in range(N - 1):
+            total = total + rj[h, d].astype(F32)
+        gi_ref[:, h * (E // 2):(h + 1) * (E // 2)] = total
     add_b(2)
 
 
@@ -531,7 +553,8 @@
         V((COLOURS, N // XL, N, XL, N, rows, CW), BF16), V((N - 1, N, N, rows, CW), BF16),
         V((N - 1, N // XL, N, XL, rows, CW), BF16), V((N - 1, N // XL, XL, N, rows, CW), BF16),
         V((COLOURS, N * N, rows, CW), BF16), V((COLOURS, N * N - 1, rows, CW), BF16),
-        V((N, N, rows, E), BF16), V((N * N - 1, rows, E), BF16),
+        V((N, N, rows, E), BF16), V((2, N - 1, N, rows, E // 2), BF16),
+        V((2, N, rows, E // 2), BF16), V((2, N - 1, rows, E // 2), BF16),
         V((3, N, 8, 128), F32), V((CORES, 8, 128), F32),
         V((1, 1), F32), V((1, 1), F32), V((1, users), jnp.int32), V((1, users), jnp.int32),
         dma(8), dma(QN), dma(QN), dma(N * CORES - 1, N // XL), dma(N * CORES - 1, N // XL),
@@ -539,7 +562,7 @@
         dma(NS - 1), dma(NS - 1), dma(NU - 1), dma(NU - 1),
         dma(NS - 1), dma(NS - 1), dma(NU - 1), dma(NU - 1), dma(COLOURS, users // 8), dma(COLOURS, users // 8), dma(N), dma(N), dma(N), dma(N),
         dma(COLOURS, N - 1), dma(COLOURS, N - 1), dma(COLOURS, N * N - 1), dma(COLOURS, N * N - 1),
-        dma(N * N - 1), dma(N * N - 1), dma(3, N - 1), dma(3, N - 1), dma(4), dma(4),
+        dma(2, N - 1), dma(2, N - 1), dma(2, N - 1), dma(2, N - 1), dma(3, N - 1), dma(3, N - 1), dma(4), dma(4),
     ]
     outs = pl.pallas_call(
         functools.partial(tower_kernel, N, XL, total),

time: 55.4 us -> 55 us (level); the launches traced: 55.3 us -> 54 us
  Pallas kernels: 53.3 us -> 52.1 us
    pallas_call x1, Pallas kernels: 52.7 us -> 51.4 us  [shards(): pl.pallas_call(functools.partial(tower_kernel, N, XL, total), name='two_t...]
where the time goes in v8:
time: 55 us; the launch traced here: 54 us
  Pallas kernels  52.1 us (95%)
  between operations  1.93 us (4%)
    pallas_call x1, Pallas kernels, shards(): pl.pallas_call(functools.partial(tower_kernel, N, XL, total), name='two_t...  51.4 us

profile of v8, /device:TPU:0, one launch (start us, length us, event | category | flops | bytes accessed | tf_op | source)
XLA Modules:
  0.0 54.0 jit_solution(2196613081239739125)
XLA Ops:
  1.9 51.4 %two_tower.1 = (f32[8,128]{1,0:T(8,128)S(1)}, f32[32,768]{1,0:T(8,128)S(1)}, f32[16,768]{1,0:T(8,128)S(1)}, f32[16,768]{1,0:T(8,128)S(1)}) custom-call(bf16[768,2048]{1,0:T(8,128)(2,1)} %bitcast.7, bf16[32,2048]{1,0:T(8,128)(2,1)} %ci_hbm.1, bf16[2048,768]{1,0:T(8,128)(2,1)} %wu_hbm.1, bf16[2048,768]{1,0:T(8,128)(2,1)} %wi_hbm.1, f32[1,1]{1,0:T(1,128)} %bitcast.5.scale_ref, ...), custom_call_target="tpu_custom_call" | custom-call | tf_op jit(solution)/shard_map/two_tower/pallas_call | solution.py:567
  53.3 0.7 %hand_out.1 = (f32[1]{0:T(128)}, f32[32,768]{1,0:T(8,128)}, f32[16,768]{1,0:T(8,128)}, f32[16,768]{1,0:T(8,128)}) custom-call(f32[8,128]{1,0:T(8,128)S(1)} %get-tuple-element.8.loss, f32[32,768]{1,0:T(8,128)S(1)} %get-tuple-element.9.ig, f32[16,768]{1,0:T(8,128)S(1)} %get-tuple-element.10.gu, f32[16,768]{1,0:T(8,128)S(1)} %get-tuple-element.11.gi), custom_call_target="tpu_custom_call" | custom-call | tf_op jit(solution)/shard_map/hand_out/pallas_call | solution.py:586

commit v9 on v8

--- a/solution.py
+++ b/solution.py
@@ -182,12 +182,34 @@
         x_recv.append(send(xv.at[:, cols], xs.at[q], xsem_s.at[q], xsem_r.at[q], sibling))
     load_wu.wait()
 
+    def pool(n, u):
+        cols = pl.ds(pl.multiple_of(n * CW, CW), CW)
+        v = pre[pl.ds(pl.multiple_of(u * 8 * HIST, 8 * HIST), 8 * HIST), cols]
+        act = v * sigmoid(v)
+        pooled[pl.ds(pl.multiple_of(u * 8, 8), 8), cols] = jnp.sum(act.reshape(8, HIST, CW), axis=1) / HIST
+
     def forward(n, _):
-        cols = pl.ds(pl.multiple_of(n * 256, 256), 256)
+        for u in range(USERS // 8):
+            pool(jnp.maximum(n - 1, 0), u)
+        cols = pl.ds(pl.multiple_of(n * CW, CW), CW)
         pre[:, cols] = dot(xv[...], wuv[:, cols])
         return 0
 
-    lax.fori_loop(0, E // 256, forward, 0)
+    lax.fori_loop(0, COLOURS, forward, 0)
+    def pool_last(u, _):
+        pool(COLOURS - 1, u)
+        return 0
+
+    lax.fori_loop(0, USERS // 8, pool_last, 0)
+    mean = pooled[...]
+    user_len = jnp.sqrt(jnp.sum(mean * mean, axis=1, keepdims=True) + EPS)
+    user_normed = mean / user_len
+    ulen[...] = jnp.broadcast_to(user_len, (USERS, 128))
+    pooled[...] = user_normed
+    ua[my_user_slot] = user_normed.astype(BF16)
+    ua_recv = []
+    for n, d in enumerate(user_peers):
+        ua_recv.append(send(ua.at[my_user_slot], ua.at[my_user_slot], ua_s.at[n], ua_r.at[n], user_peer(*d)))
 
     for copy in slot_recv + id_recv:
         copy.wait_recv()
@@ -213,25 +235,6 @@
     tgt_recv = []
     for n, d in enumerate(user_peers):
         tgt_recv.append(send(tgtbuf.at[0], tgtbuf.at[n + 1], tgt_s.at[n], tgt_r.at[n], user_peer(*d)))
-
-    def pool(n, _):
-        u = n // COLOURS
-        cols = pl.ds(pl.multiple_of(lax.rem(n, COLOURS) * CW, CW), CW)
-        v = pre[pl.ds(pl.multiple_of(u * 8 * HIST, 8 * HIST), 8 * HIST), cols]
-        act = v * sigmoid(v)
-        pooled[pl.ds(pl.multiple_of(u * 8, 8), 8), cols] = jnp.sum(act.reshape(8, HIST, CW), axis=1) / HIST
-        return 0
-
-    lax.fori_loop(0, (USERS // 8) * COLOURS, pool, 0)
-    mean = pooled[...]
-    user_len = jnp.sqrt(jnp.sum(mean * mean, axis=1, keepdims=True) + EPS)
-    user_normed = mean / user_len
-    ulen[...] = jnp.broadcast_to(user_len, (USERS, 128))
-    pooled[...] = user_normed
-    ua[my_user_slot] = user_normed.astype(BF16)
-    ua_recv = []
-    for n, d in enumerate(user_peers):
-        ua_recv.append(send(ua.at[my_user_slot], ua.at[my_user_slot], ua_s.at[n], ua_r.at[n], user_peer(*d)))
 
     xi_recv = []
     for n, (dz, dc) in enumerate(feat_peers):

time: 55 us -> 51.9 us (0.944); the launches traced: 54 us -> 51.6 us
  Pallas kernels: 52.1 us -> 49.7 us
    pallas_call x1, Pallas kernels: 51.4 us -> 49 us  [shards(): pl.pallas_call(functools.partial(tower_kernel, N, XL, total), name='two_t...]
where the time goes in v9:
time: 51.9 us; the launch traced here: 51.6 us
  Pallas kernels  49.7 us (96%)
  between operations  1.93 us (4%)
    pallas_call x1, Pallas kernels, shards(): pl.pallas_call(functools.partial(tower_kernel, N, XL, total), name='two_t...  49 us

profile of v9, /device:TPU:0, one launch (start us, length us, event | category | flops | bytes accessed | tf_op | source)
XLA Modules:
  0.0 51.6 jit_solution(13291373958485915623)
XLA Ops:
  1.9 49.0 %two_tower.1 = (f32[8,128]{1,0:T(8,128)S(1)}, f32[32,768]{1,0:T(8,128)S(1)}, f32[16,768]{1,0:T(8,128)S(1)}, f32[16,768]{1,0:T(8,128)S(1)}) custom-call(bf16[768,2048]{1,0:T(8,128)(2,1)} %bitcast.7, bf16[32,2048]{1,0:T(8,128)(2,1)} %ci_hbm.1, bf16[2048,768]{1,0:T(8,128)(2,1)} %wu_hbm.1, bf16[2048,768]{1,0:T(8,128)(2,1)} %wi_hbm.1, f32[1,1]{1,0:T(1,128)} %bitcast.5.scale_ref, ...), custom_call_target="tpu_custom_call" | custom-call | tf_op jit(solution)/shard_map/two_tower/pallas_call | solution.py:570
  50.9 0.7 %hand_out.1 = (f32[1]{0:T(128)}, f32[32,768]{1,0:T(8,128)}, f32[16,768]{1,0:T(8,128)}, f32[16,768]{1,0:T(8,128)}) custom-call(f32[8,128]{1,0:T(8,128)S(1)} %get-tuple-element.8.loss, f32[32,768]{1,0:T(8,128)S(1)} %get-tuple-element.9.ig, f32[16,768]{1,0:T(8,128)S(1)} %get-tuple-element.10.gu, f32[16,768]{1,0:T(8,128)S(1)} %get-tuple-element.11.gi), custom_call_target="tpu_custom_call" | custom-call | tf_op jit(solution)/shard_map/hand_out/pallas_call | solution.py:589

commit v10 on v9

--- a/solution.py
+++ b/solution.py
@@ -36,7 +36,7 @@
     x_hbm, ci_hbm, wu_hbm, wi_hbm, scale_ref, shift_ref, ids_ref, slot_ref,
     loss_ref, ig_ref, gu_ref, gi_ref,
     xv, xs, civ, wuv, wiv, pre, pooled, gp, ulen, inorm, ilen,
-    ua, ia, idrow, idbuf, slotbuf, tgtbuf, wt, pig, pigf, rigc, rig, pgu, rgu, g, gi, xi, xt,
+    ua, ia, idrow, idbuf, slotbuf, tgtbuf, sc, wt, pig, pigf, rigc, rig, pgu, rgu, g, gi, xi, xt,
     part, ra0, ra1, ra2, sa, rb, parti, ri, si, rj, losses, corelosses, scale_s, shift_s, idv, slotv,
     lsem, xsem_s, xsem_r, xi_s, xi_r, id_s, id_r, slot_s, slot_r, tgt_s, tgt_r,
     ia_s, ia_r, ua_s, ua_r, ig_s, ig_r, ug_s, ug_r, g_s, g_r, gi_s, gi_r, gh_s, gh_r,
@@ -260,22 +260,24 @@
         return 0
 
     lax.fori_loop(0, QN, turn, 0)
+    for copy in ua_recv:
+        copy.wait_recv()
+    ia_hop.wait_recv()
+    users = ua[...].reshape(NU * USERS, E)
+    for n in range(NI // N):
+        items = ia[n // 2, (n % 2) * N:(n % 2 + 1) * N].reshape(N * USERS, E)
+        sc[n * N * USERS:(n + 1) * N * USERS, :] = dot_nt(items, users)
     for copy in tgt_recv:
         copy.wait_recv()
     targets = tgtbuf[0]
     for n in range(1, NU):
         targets = targets + tgtbuf[n]
 
-    for copy in ua_recv:
-        copy.wait_recv()
-    ia_hop.wait_recv()
     scale = scale_s[0, 0]
     shift = shift_s[0, 0]
-    users = ua[...].reshape(NU * USERS, E)
     loss = jnp.zeros((8, 128), F32)
     for n in range(NI // N):
-        items = ia[n // 2, (n % 2) * N:(n % 2 + 1) * N].reshape(N * USERS, E)
-        scores = dot_nt(items, users)
+        scores = sc[n * N * USERS:(n + 1) * N * USERS, :]
         ids = idbuf[n * N:(n + 1) * N].reshape(N * USERS, 128)
         sign = jnp.where(jnp.concatenate([ids] * wide, axis=1) == targets, 1.0, -1.0)
         margin = sign * (scale * scores + shift)
@@ -547,7 +549,7 @@
         V((users, E), F32), V((users, 128), F32),
         V((NU, users, E), BF16), V((CORES, NS, users, E), BF16), V((NI, 1, 128), F32), V((NI, users, 128), F32),
         V((NU, 1, NU * users), F32), V((NU, 1, NU * users), F32),
-        V((NI * users, NU * users), BF16),
+        V((NI * users, NU * users), F32), V((NI * users, NU * users), BF16),
         V((CORES, NS, users, E), BF16), V((NS, users, E), F32), V((NS, users, E), BF16),
         V((NS - 1, users, E), BF16),
         V((NU, users, E), BF16), V((NU - 1, users, E), BF16),

time: 51.9 us -> 52 us (level)
  no operation moved by 1% of the time
where the time goes in v10:
time: 52 us; the launch traced here: 51.8 us
  Pallas kernels  49.8 us (96%)
  between operations  1.93 us (4%)
    pallas_call x1, Pallas kernels, shards(): pl.pallas_call(functools.partial(tower_kernel, N, XL, total), name='two_t...  49.1 us

profile of v10, /device:TPU:0, one launch (start us, length us, event | category | flops | bytes accessed | tf_op | source)
XLA Modules:
  0.0 51.8 jit_solution(1838751385947595487)
XLA Ops:
  1.9 49.1 %two_tower.1 = (f32[8,128]{1,0:T(8,128)S(1)}, f32[32,768]{1,0:T(8,128)S(1)}, f32[16,768]{1,0:T(8,128)S(1)}, f32[16,768]{1,0:T(8,128)S(1)}) custom-call(bf16[768,2048]{1,0:T(8,128)(2,1)} %bitcast.7, bf16[32,2048]{1,0:T(8,128)(2,1)} %ci_hbm.1, bf16[2048,768]{1,0:T(8,128)(2,1)} %wu_hbm.1, bf16[2048,768]{1,0:T(8,128)(2,1)} %wi_hbm.1, f32[1,1]{1,0:T(1,128)} %bitcast.5.scale_ref, ...), custom_call_target="tpu_custom_call" | custom-call | tf_op jit(solution)/shard_map/two_tower/pallas_call | solution.py:572
  51.1 0.7 %hand_out.1 = (f32[1]{0:T(128)}, f32[32,768]{1,0:T(8,128)}, f32[16,768]{1,0:T(8,128)}, f32[16,768]{1,0:T(8,128)}) custom-call(f32[8,128]{1,0:T(8,128)S(1)} %get-tuple-element.8.loss, f32[32,768]{1,0:T(8,128)S(1)} %get-tuple-element.9.ig, f32[16,768]{1,0:T(8,128)S(1)} %get-tuple-element.10.gu, f32[16,768]{1,0:T(8,128)S(1)} %get-tuple-element.11.gi), custom_call_target="tpu_custom_call" | custom-call | tf_op jit(solution)/shard_map/hand_out/pallas_call | solution.py:591
